TPU v7x, 32 devices: a whole 2x2x4 slice. The times are simulated.
32 devices in a mesh: chain: 8 (over z, core), dp: 4 (over y, x).
Axes of the slice: x: 2, y: 2, z: 4, core: 2. Of those that a mesh axis runs over, the one named last changes fastest.
Arguments:
- images_in: float32 [8, 1024, 1024], P('chain', 'dp'), may hold values from -8 to 8
- images_mid: float32 [8, 1024, 1024], P('chain', 'dp'), may hold values from -8 to 8
- images_out: float32 [8, 1024, 1000], P('chain', 'dp'), may hold values from -8 to 8
- ends_in: float32 [2, 1024, 1024], P(None, 'dp'), may hold values from -8 to 8
- ends_mid: float32 [2, 1024, 1024], P(None, 'dp'), may hold values from -8 to 8
- ends_out: float32 [2, 1024, 1000], P(None, 'dp'), may hold values from -8 to 8
- data_pool: bfloat16 [7168, 1024], P('dp'), may hold values from -6 to 6
- batch_rows: int32 [8, 3584], P('chain', 'dp'), may hold values from 0 to 1791
- labels: int32 [8, 3584], P('chain', 'dp'), may hold values from 0 to 999
- climbing: int32 [8], P('chain'), may hold values 0 or 1
Outputs:
- new_in: float32 [8, 1024, 1024], P('chain', 'dp')
- new_mid: float32 [8, 1024, 1024], P('chain', 'dp')
- new_out: float32 [8, 1024, 1000], P('chain', 'dp')
- energies: float32 [8], P('chain')
- arc_share: float32 [8], P('chain')
- bend: float32 [8], P('chain')
Inputs may be any that keep to these rules, and one draw needn't show every extreme that they name: batch_rows[i, b] names a row of the pool shard held by dp index b // 896.
All inputs are finite; a program needn't handle non-finite values. No bound on the sum of `climbing` on one device may be relied on, other than what follows from the above.
Results may differ from a plain program's by a relative error of at most 0.0023.
Values may be sent and summed in bfloat16 or wider, within the bound.
A program may use at most 128 MiB of HBM per device.

v0:
```python
import jax
import jax.numpy as jnp
from jax import lax
from jax.sharding import PartitionSpec as P

SPRING = 0.03
EPS = 1e-06


def for_sending(value):

    def short(part):
        return part.astype(jnp.bfloat16) if part.dtype == jnp.float32 else part

    return jax.tree.map(short, value)


def passed_along(block, axis, distance):
    devices = range(lax.axis_size(axis))
    route = [(i - distance, i) for i in devices if i - distance in devices]
    return lax.ppermute(block, axis, route)


def prefix(value, axis, combine, identity):
    peers, mine = (lax.axis_size(axis), lax.axis_index(axis))
    everything = lax.all_gather(value, axis)
    start = jnp.broadcast_to(jnp.asarray(identity, value.dtype), value.shape)

    def step(k, before):
        reached = k < mine
        new = combine(before, everything[k])
        return jnp.where(reached, new, before)

    return lax.fori_loop(0, peers, step, start)


def silu_slope(pre):
    sig = jax.nn.sigmoid(pre)
    return sig * (1.0 + pre * (1.0 - sig))


def dot_nt(left, right):
    return lax.dot_general(
        left, right, (((1,), (1,)), ((), ())), preferred_element_type=jnp.float32
    )


def dot_tn(left, right):
    return lax.dot_general(
        left, right, (((0,), (0,)), ((), ())), preferred_element_type=jnp.float32
    )


def inner(first, second):
    total = jnp.float32(0.0)
    for left, right in zip(first, second):
        total = total + jnp.sum(left * right)
    return total


def on_device(
    images_in,
    images_mid,
    images_out,
    ends_in,
    ends_mid,
    ends_out,
    data_pool,
    batch_rows,
    labels,
    climbing,
):
    own = (images_in[0], images_mid[0], images_out[0])
    width = data_pool.shape[1]
    hidden_units = images_in.shape[2]
    classes = images_out.shape[2]
    groups = lax.axis_size("dp")
    factors = (width ** (-0.5), hidden_units ** (-0.5), width ** (-0.5))
    lowered = tuple(((p * f).astype(jnp.bfloat16) for p, f in zip(own, factors)))
    w_in, w_mid, w_out = jax.tree.map(
        lambda part, own: part.astype(own.dtype),
        lax.all_gather(for_sending(lowered), "dp", axis=0, tiled=True),
        lowered,
    )
    rows = data_pool[batch_rows[0]]
    batch = rows.shape[0] * groups
    pre = jnp.dot(rows, w_in, preferred_element_type=jnp.float32)
    hid = jax.nn.silu(pre).astype(jnp.bfloat16)
    resid = (
        rows.astype(jnp.float32) + jnp.dot(hid, w_mid, preferred_element_type=jnp.float32)
    ).astype(jnp.bfloat16)
    logits = jnp.dot(resid, w_out, preferred_element_type=jnp.float32)
    target = (labels[0][:, None] == jnp.arange(classes, dtype=jnp.int32)[None, :]).astype(
        jnp.float32
    )
    err = logits - target
    norm = 1.0 / (batch * classes)
    energy_part = 0.5 * norm * jnp.sum(err * err)
    d_logits = (err * norm).astype(jnp.bfloat16)
    d_resid = dot_nt(d_logits, w_out).astype(jnp.bfloat16)
    d_pre = (dot_nt(d_resid, w_mid) * silu_slope(pre)).astype(jnp.bfloat16)
    summed = (
        lax.psum_scatter(
            dot_tn(rows, d_pre).astype(jnp.bfloat16), "dp", scatter_dimension=0, tiled=True
        ).astype(jnp.float32),
        lax.psum_scatter(
            dot_tn(hid, d_resid).astype(jnp.bfloat16), "dp", scatter_dimension=0, tiled=True
        ).astype(jnp.float32),
        lax.psum_scatter(
            dot_tn(resid, d_logits).astype(jnp.bfloat16), "dp", scatter_dimension=0, tiled=True
        ).astype(jnp.float32),
    )
    grads = tuple((g * f for g, f in zip(summed, factors)))
    index = lax.axis_index("chain")
    count = lax.axis_size("chain")
    ends = (ends_in, ends_mid, ends_out)
    left = (
        passed_along(own[0].astype(jnp.bfloat16), "chain", 1).astype(jnp.float32),
        passed_along(own[1].astype(jnp.bfloat16), "chain", 1).astype(jnp.float32),
        passed_along(own[2].astype(jnp.bfloat16), "chain", 1).astype(jnp.float32),
    )
    right = (
        passed_along(own[0].astype(jnp.bfloat16), "chain", -1).astype(jnp.float32),
        passed_along(own[1].astype(jnp.bfloat16), "chain", -1).astype(jnp.float32),
        passed_along(own[2].astype(jnp.bfloat16), "chain", -1).astype(jnp.float32),
    )
    left = tuple((jnp.where(index == 0, e[0], piece) for e, piece in zip(ends, left)))
    right = tuple((jnp.where(index == count - 1, e[1], piece) for e, piece in zip(ends, right)))
    ahead = tuple((r - o for r, o in zip(right, own)))
    behind = tuple((o - l for o, l in zip(own, left)))
    sq_ahead, sq_behind, cross, g_ahead, g_behind, g_g, energy = lax.psum(
        (
            inner(ahead, ahead),
            inner(behind, behind),
            inner(ahead, behind),
            inner(grads, ahead),
            inner(grads, behind),
            inner(grads, grads),
            energy_part,
        ),
        "dp",
    )
    len_ahead = jnp.sqrt(sq_ahead + EPS)
    len_behind = jnp.sqrt(sq_behind + EPS)
    raw_sq = (
        sq_ahead / (len_ahead * len_ahead)
        + sq_behind / (len_behind * len_behind)
        + 2.0 * cross / (len_ahead * len_behind)
    )
    raw_len = jnp.sqrt(raw_sq + EPS)
    tau = tuple(((a / len_ahead + b / len_behind) / raw_len for a, b in zip(ahead, behind)))
    along = (g_ahead / len_ahead + g_behind / len_behind) / raw_len
    tau_sq = raw_sq / (raw_sq + EPS)
    earlier = prefix(len_behind, "chain", lambda first, later: first + later, jnp.float32(0.0))
    arc = earlier + len_behind
    band = lax.psum(len_behind + jnp.where(index == count - 1, len_ahead, 0.0), "chain")
    goal = (index + 1).astype(jnp.float32) / (count + 1) * band
    coef = jnp.where(climbing[0] == 1, 2.0 * along, along + SPRING * (goal - arc) / band)
    force = tuple((-g + coef * t for g, t in zip(grads, tau)))
    force_sq = g_g - 2.0 * coef * along + coef * coef * tau_sq
    scale = band / (count + 1) / jnp.sqrt(force_sq + EPS)
    new = tuple(((o + scale * f)[None] for o, f in zip(own, force)))
    return (new[0], new[1], new[2], energy[None], (arc / band)[None], (0.5 * raw_len)[None])


def solution(mesh):
    placed = (
        P("chain", "dp", None),
        P("chain", "dp", None),
        P("chain", "dp", None),
        P(None, "dp", None),
        P(None, "dp", None),
        P(None, "dp", None),
        P("dp", None),
        P("chain", "dp"),
        P("chain", "dp"),
        P("chain"),
    )
    return jax.shard_map(
        on_device,
        mesh=mesh,
        in_specs=placed,
        out_specs=(
            P("chain", "dp", None),
            P("chain", "dp", None),
            P("chain", "dp", None),
            P("chain"),
            P("chain"),
            P("chain"),
        ),
        check_vma=False,
    )
```

profile of v0, /device:TPU:0, one launch (start us, length us, event | category | flops | bytes accessed | tf_op | source)
XLA Modules:
  0.0 320.3 jit_solution(3289639381327560830)
XLA Ops:
  7.2 2.2 fusion.6
  9.5 0.0 all-gather.6.cloned.1.call-start
  9.6 0.9 fusion.3
  10.5 0.0 all-gather.8.cloned.1.call-start
  10.5 0.9 fusion.10
  11.4 0.0 reduce-scatter.8.cloned.1.call-start
  11.5 8.1 %gather_fusion = bf16[896,1024]{1,0:T(8,128)(2,1)} fusion(bf16[1792,1024]{1,0:T(8,128)(2,1)} %param.18, s32[1024]{0:T(1024)S(1)} %pad_clamp_fusion), kind=kCustom, calls=%fused_computation | custom fusion | bytes 3673600 | tf_op jit(solution)/shard_map/gather | solution.py:85
  19.6 28.7 %all-gather.4.cloned.1.call-done = bf16[1024,1024]{1,0:T(8,128)(2,1)} async-done(((bf16[256,1024]{1,0:T(8,128)(2,1)}), bf16[1024,1024]{1,0:T(8,128)(2,1)}) %all-gather.4.cloned.1.call-update) | async-done | bytes 2097168 | tf_op jit(solution)/shard_map/all_gather | solution.py:82
  48.3 6.0 %fusion.22 = f32[896,1024]{1,0:T(8,128)} fusion(bf16[896,1024]{1,0:T(8,128)(2,1)} %gather_fusion, bf16[1024,1024]{1,0:T(8,128)(2,1)} %all-gather.4.cloned.1.call-done), kind=kOutput, calls=%fused_computation.67 | convolution fusion | flops 1879048192 | bytes 7602176 | tf_op jit(solution)/shard_map/dot_general | solution.py:87
  54.4 31.6 %all-gather.6.cloned.1.call-done = bf16[1024,1024]{1,0:T(8,128)(2,1)} async-done(((bf16[256,1024]{1,0:T(8,128)(2,1)}), bf16[1024,1024]{1,0:T(8,128)(2,1)}) %all-gather.6.cloned.1.call-update) | async-done | bytes 2097168 | tf_op jit(solution)/shard_map/all_gather | solution.py:82
  86.0 6.6 %add_convert_fusion = bf16[896,1024]{1,0:T(8,128)(2,1)} fusion(bf16[896,1024]{1,0:T(8,128)(2,1)} %gather_fusion, bf16[1024,1024]{1,0:T(8,128)(2,1)} %all-gather.6.cloned.1.call-done, f32[896,1024]{1,0:T(8,128)} %fusion.22), kind=kOutput, calls=%fused_computation.2 | convolution fusion | flops 1886388224 | bytes 9437184 | tf_op jit(solution)/shard_map/dot_general | solution.py:90
  92.6 30.5 %all-gather.8.cloned.1.call-done = bf16[1024,1000]{0,1:T(8,128)(2,1)} async-done(((bf16[256,1000]{0,1:T(8,128)(2,1)}), bf16[1024,1000]{0,1:T(8,128)(2,1)}) %all-gather.8.cloned.1.call-update) | async-done | bytes 2048016 | tf_op jit(solution)/shard_map/all_gather | solution.py:82
  123.1 5.3 %multiply_reduce_fusion = (f32[]{:T(128)}, f32[896,1000]{0,1:T(8,128)S(1)}) fusion(s32[896]{0:T(1024)S(1)} %reduce.1, bf16[896,1024]{1,0:T(8,128)(2,1)} %add_convert_fusion, bf16[1024,1000]{0,1:T(8,128)(2,1)} %all-gather.8.cloned.1.call-done), kind=kOutput, calls=%fused_computation.5 | convolution fusion | flops 1839488000 | bytes 7470596 | tf_op jit(solution)/shard_map/dot_general | solution.py:92
  128.4 1.8 copy-done.10
  130.2 3.6 %convolution_convert_fusion.2 = bf16[1024,1000]{0,1:T(8,128)(2,1)} fusion(bf16[896,1024]{1,0:T(8,128)(2,1)S(1)} %copy-done.11, f32[896,1000]{0,1:T(8,128)S(1)} %get-tuple-element.128, s32[896]{0:T(1024)S(1)} %reduce.1), kind=kOutput, calls=%fused_computation.11 | convolution fusion | flops 1840512000 | bytes 7470592 | tf_op jit(solution)/shard_map/dot_general | solution.py:49
  133.9 0.2 reduce-scatter.4.cloned.1.call-start
  134.1 6.1 %convolution_convert_fusion.3 = bf16[896,1024]{1,0:T(8,128)(2,1)} fusion(bf16[1024,1000]{0,1:T(8,128)(2,1)} %all-gather.8.cloned.1.call-done, f32[896,1000]{0,1:T(8,128)} %copy-done.10, s32[896]{0:T(1024)S(1)} %reduce.1), kind=kOutput, calls=%fused_computation.12 | convolution fusion | flops 1840405504 | bytes 7470592 | tf_op jit(solution)/shard_map/dot_general | solution.py:43
  140.2 9.9 %convolution_convert_fusion.1 = bf16[1024,1024]{1,0:T(8,128)(2,1)} fusion(bf16[896,1024]{1,0:T(8,128)(2,1)} %gather_fusion, f32[896,1024]{1,0:T(8,128)} %fusion.22, bf16[896,1024]{1,0:T(8,128)(2,1)} %convolution_convert_fusion.3, bf16[1024,1024]{1,0:T(8,128)(2,1)} %all-gather.6.cloned.1.call-done), kind=kOutput, calls=%fused_computation.10 | convolution fusion | flops 3767402496 | bytes 11534336 | tf_op jit(solution)/shard_map/dot_general | solution.py:49
  150.1 6.4 %convolution_convert_fusion = bf16[1024,1024]{1,0:T(8,128)(2,1)} fusion(bf16[896,1024]{1,0:T(8,128)(2,1)} %convolution_convert_fusion.3, f32[896,1024]{1,0:T(8,128)} %fusion.22), kind=kOutput, calls=%fused_computation.9 | convolution fusion | flops 1884684288 | bytes 7602176 | tf_op jit(solution)/shard_map/dot_general | solution.py:49
  156.6 0.8 bitcast_convert_fusion.2
  157.4 2.7 collective-permute-start.2
  160.1 1.3 collective-permute-start.5
  161.4 0.9 bitcast_convert_fusion.1
  162.2 4.4 %collective-permute-start = (bf16[256,1024]{1,0:T(8,128)(2,1)}, bf16[256,1024]{1,0:T(8,128)(2,1)}, u32[]{:S(2)}, u32[]{:S(2)}) collective-permute-start(bf16[256,1024]{1,0:T(8,128)(2,1)} %bitcast_convert_fusion.1), channel_id=1, source_target_pairs={{0,4},{4,8},{8,12},{12,16},{16,20},{20,24},{24,28},{1,5},{5,9},{9,... | collective-permute-start | bytes 1572872 | tf_op jit(solution)/shard_map/ppermute | solution.py:21
  166.6 1.3 collective-permute-start.3
  167.9 0.9 bitcast_convert_fusion
  168.8 4.3 %collective-permute-start.1 = (bf16[256,1024]{1,0:T(8,128)(2,1)}, bf16[256,1024]{1,0:T(8,128)(2,1)}, u32[]{:S(2)}, u32[]{:S(2)}) collective-permute-start(bf16[256,1024]{1,0:T(8,128)(2,1)} %bitcast_convert_fusion), channel_id=1, source_target_pairs={{0,4},{4,8},{8,12},{12,16},{16,20},{20,24},{24,28},{1,5},{5,9},{9,... | collective-permute-start | bytes 1572872 | tf_op jit(solution)/shard_map/ppermute | solution.py:21
  173.7 0.6 dynamic-slice
  175.1 1.5 collective-permute-start.4
  176.6 4.6 %multiply_reduce_fusion.14 = (f32[]{:T(128)}, f32[]{:T(128)}, f32[]{:T(128)}, f32[]{:T(128)}, f32[]{:T(128)}, /*index=5*/f32[]{:T(128)}, f32[256,1000]{0,1:T(8,128)}, f32[256,1000]{0,1:T(8,128)}) fusion(bf16[256,1000]{0,1:T(8,128)(2,1)} %reduce-scatter.8.cloned.1.call-done, f32[1,256,1000]{1,2,0:T(8,128)S(1)} %copy-done.2, ...), kind=kLoop, calls=%fused_computation.55 | loop fusion | flops 5119994 | bytes 6656026 | tf_op jit(solution)/shard_map/reduce_sum | solution.py:57
  181.2 26.2 %reduce-scatter.4.cloned.1.call-done = bf16[256,1024]{1,0:T(8,128)(2,1)} async-done(((bf16[1024,1024]{1,0:T(8,128)(2,1)}), bf16[256,1024]{1,0:T(8,128)(2,1)}) %reduce-scatter.4.cloned.1.call-update) | async-done | bytes 524304 | tf_op jit(solution)/shard_map/reduce_scatter | solution.py:103
  207.5 4.7 %multiply_reduce_fusion.4 = (f32[]{:T(128)}, f32[]{:T(128)}, f32[]{:T(128)}, f32[]{:T(128)}, f32[]{:T(128)}, /*index=5*/f32[]{:T(128)}, f32[256,1024]{1,0:T(8,128)}, f32[256,1024]{1,0:T(8,128)}) fusion(bf16[256,1024]{1,0:T(8,128)(2,1)} %reduce-scatter.4.cloned.1.call-done, f32[1,256,1024]{2,1,0:T(8,128)S(1)} %copy-done.1, ...), kind=kLoop, calls=%fused_computation.34 | loop fusion | flops 5242874 | bytes 6815770 | tf_op jit(solution)/shard_map/reduce_sum | solution.py:57
  212.2 33.3 %reduce-scatter.6.cloned.1.call-done = bf16[256,1024]{1,0:T(8,128)(2,1)} async-done(((bf16[1024,1024]{1,0:T(8,128)(2,1)}), bf16[256,1024]{1,0:T(8,128)(2,1)}) %reduce-scatter.6.cloned.1.call-update) | async-done | bytes 524304 | tf_op jit(solution)/shard_map/reduce_scatter | solution.py:106
  245.5 4.7 %multiply_reduce_fusion.3 = (f32[]{:T(128)}, f32[]{:T(128)}, f32[]{:T(128)}, f32[]{:T(128)}, f32[]{:T(128)}, /*index=5*/f32[]{:T(128)}, f32[256,1024]{1,0:T(8,128)}, f32[256,1024]{1,0:T(8,128)}) fusion(bf16[256,1024]{1,0:T(8,128)(2,1)} %reduce-scatter.6.cloned.1.call-done, f32[1,256,1024]{2,1,0:T(8,128)S(1)} %copy-done, ...), kind=kLoop, calls=%fused_computation.33 | loop fusion | flops 5242874 | bytes 6815770 | tf_op jit(solution)/shard_map/reduce_sum | solution.py:57
  261.4 10.2 %all-reduce.2 = (f32[]{:T(128)}, f32[]{:T(128)}, f32[]{:T(128)}, f32[]{:T(128)}, f32[]{:T(128)}, /*index=5*/f32[]{:T(128)}, f32[1]{0:T(128)}) all-reduce(f32[]{:T(128)S(6)} %add.178, f32[]{:T(128)S(6)} %add.175, f32[]{:T(128)S(6)} %add.195, f32[]{:T(128)S(6)} %add.189, f32[]{:T(128)S(6)} %add.191, ...), channel_id=1, replica_groups=mesh['chain'=8,'dp'=4] {'dp'}, use_global_device_ids=true, to_apply=%region_7.8 | all-reduce | flops 7 | bytes 56 | tf_op jit(solution)/shard_map/psum | solution.py:131
  274.9 0.7 dynamic-update-slice
  275.7 14.6 %all-reduce.1 = (f32[]{:T(128)}, f32[8]{0:T(128)S(1)}) all-reduce(f32[]{:T(128)S(6)} %add.180, f32[8]{0:T(128)S(1)} %dynamic-update-slice), channel_id=1, replica_groups=mesh['chain'=8,'dp'=4] {'chain'}, use_global_device_ids=true, to_apply=%region_8.9 | all-reduce | flops 9 | bytes 72 | tf_op jit(solution)/shard_map/psum | solution.py:156
  290.3 10.0 %while.13 = (s32[]{:T(128)}, f32[]{:T(128)}, s32[]{:T(128)}, f32[8]{0:T(128)S(1)}, s32[]{:T(128)}) while((s32[]{:T(128)}, f32[]{:T(128)}, s32[]{:T(128)}, f32[8]{0:T(128)S(1)}, s32[]{:T(128)}) %tuple.55), condition=%wide.region_29.30_spmd, body=%wide.region_28.29_spmd.sunk | while | flops 5 | bytes 107 | solution.py:34
  290.3 0.6 dynamic_slice.8
  291.6 0.6 dynamic_slice.8
  292.8 0.6 dynamic_slice.8
  294.1 0.6 dynamic_slice.8
  295.3 0.6 dynamic_slice.8
  296.6 0.6 dynamic_slice.8
  297.8 0.6 dynamic_slice.8
  299.1 0.6 dynamic_slice.8
  304.6 3.1 fusion.11
  307.7 3.4 %fusion.4 = (f32[1,256,1024]{2,1,0:T(8,128)}, f32[1,256,1024]{2,1,0:T(8,128)}) fusion(f32[1,256,1024]{2,1,0:T(8,128)S(1)} %copy-done, f32[256,1024]{1,0:T(8,128)S(1)} %copy-done.6, f32[256,1024]{1,0:T(8,128)S(1)} %copy-done.5, bf16[256,1024]{1,0:T(8,128)(2,1)} %reduce-scatter.6.cloned.1.call-done, f32[]{:T(128)S(6)} %sqrt.14, f32[]{:T(128)} %sqrt.12, ...), kind=kLoop, calls=%fused_computation.23 | loop fusion | flops 5767168 | bytes 9437204 | tf_op jit(solution)/shard_map/broadcast_in_dim | solution.py:162
  (42 shorter events, 0.3 us)
Async XLA Ops:
  7.2 2.4 copy-start
  7.2 3.4 %copy-start.2 = (f32[1,256,1000]{1,2,0:T(8,128)S(1)}, f32[1,256,1000]{1,2,0:T(8,128)}, u32[]{:S(2)}) copy-start(f32[1,256,1000]{1,2,0:T(8,128)} %param.14) | copy-start | bytes 3072004
  7.2 41.2 %all-gather.4.cloned.1.call-start = ((), (), s32[]{:S(2)}) async-start(), calls=%async_computation.3 | async-start | bytes 2621440 | tf_op jit(solution)/shard_map/all_gather | solution.py:82
  9.5 2.0 copy-start.7
  9.5 76.5 %all-gather.6.cloned.1.call-start = ((), (), s32[]{:S(2)}) async-start(), calls=%async_computation.4 | async-start | bytes 2621440 | tf_op jit(solution)/shard_map/all_gather | solution.py:82
  10.5 112.6 %all-gather.8.cloned.1.call-start = ((), (), s32[]{:S(2)}) async-start(), calls=%async_computation.5 | async-start | bytes 2560000 | tf_op jit(solution)/shard_map/all_gather | solution.py:82
  11.4 165.2 %reduce-scatter.8.cloned.1.call-start = ((), (), s32[]{:S(2)}) async-start(), calls=%async_computation.8 | async-start | bytes 2560000 | tf_op jit(solution)/shard_map/reduce_scatter | solution.py:109
  11.5 8.1 %copy-start.8 = (s32[1,896]{1,0:T(1,128)S(1)}, s32[1,896]{1,0:T(1,128)}, u32[]{:S(2)}) copy-start(s32[1,896]{1,0:T(1,128)} %param.20) | copy-start | bytes 10756
  123.0 7.1 %copy-start.11 = (bf16[896,1024]{1,0:T(8,128)(2,1)S(1)}, bf16[896,1024]{1,0:T(8,128)(2,1)}, u32[]{:S(2)}) copy-start(bf16[896,1024]{1,0:T(8,128)(2,1)} %add_convert_fusion) | copy-start | bytes 5505028
  128.4 1.8 copy-start.10
  133.9 73.6 %reduce-scatter.4.cloned.1.call-start = ((), (), s32[]{:S(2)}) async-start(), calls=%async_computation.6 | async-start | bytes 2621440 | tf_op jit(solution)/shard_map/reduce_scatter | solution.py:103
  150.0 95.5 %reduce-scatter.6.cloned.1.call-start = ((), (), s32[]{:S(2)}) async-start(), calls=%async_computation.7 | async-start | bytes 2621440 | tf_op jit(solution)/shard_map/reduce_scatter | solution.py:106
  156.5 4.8 %copy-start.1 = (f32[1,256,1024]{2,1,0:T(8,128)S(1)}, f32[1,256,1024]{2,1,0:T(8,128)}, u32[]{:S(2)}) copy-start(f32[1,256,1024]{2,1,0:T(8,128)} %param.12) | copy-start | bytes 3145732
  156.5 17.2 %copy-start.9 = (u32[32]{0:T(128)S(1)}, u32[32]{0:T(128)}, u32[]{:S(2)}) copy-start(u32[32]{0:T(128)} %constant.71) | copy-start | bytes 388
  157.4 17.7 %collective-permute-start.2 = (bf16[256,1000]{0,1:T(8,128)(2,1)}, bf16[256,1000]{0,1:T(8,128)(2,1)}, u32[]{:S(2)}, u32[]{:S(2)}) collective-permute-start(bf16[256,1000]{0,1:T(8,128)(2,1)} %bitcast_convert_fusion.2), channel_id=1, source_target_pairs={{0,4},{4,8},{8,12},{12,16},{16,20},{20,24},{24,28},{1,5},{5,9},{9,... | collective-permute-start | bytes 1536008 | tf_op jit(solution)/shard_map/ppermute | solution.py:21
  160.1 16.5 %collective-permute-start.5 = (bf16[256,1000]{0,1:T(8,128)(2,1)}, bf16[256,1000]{0,1:T(8,128)(2,1)}, u32[]{:S(2)}, u32[]{:S(2)}) collective-permute-start(bf16[256,1000]{0,1:T(8,128)(2,1)} %bitcast_convert_fusion.2), channel_id=1, source_target_pairs={{4,0},{8,4},{12,8},{16,12},{20,16},{24,20},{28,24},{5,1},{9,5},{13... | collective-permute-start | bytes 1536008 | tf_op jit(solution)/shard_map/ppermute | solution.py:21
  162.2 19.0 %collective-permute-start = (bf16[256,1024]{1,0:T(8,128)(2,1)}, bf16[256,1024]{1,0:T(8,128)(2,1)}, u32[]{:S(2)}, u32[]{:S(2)}) collective-permute-start(bf16[256,1024]{1,0:T(8,128)(2,1)} %bitcast_convert_fusion.1), channel_id=1, source_target_pairs={{0,4},{4,8},{8,12},{12,16},{16,20},{20,24},{24,28},{1,5},{5,9},{9,... | collective-permute-start | bytes 1572872 | tf_op jit(solution)/shard_map/ppermute | solution.py:21
  166.6 14.6 %collective-permute-start.3 = (bf16[256,1024]{1,0:T(8,128)(2,1)}, bf16[256,1024]{1,0:T(8,128)(2,1)}, u32[]{:S(2)}, u32[]{:S(2)}) collective-permute-start(bf16[256,1024]{1,0:T(8,128)(2,1)} %bitcast_convert_fusion.1), channel_id=1, source_target_pairs={{4,0},{8,4},{12,8},{16,12},{20,16},{24,20},{28,24},{5,1},{9,5},{13... | collective-permute-start | bytes 1572872 | tf_op jit(solution)/shard_map/ppermute | solution.py:21
  168.8 43.4 %collective-permute-start.1 = (bf16[256,1024]{1,0:T(8,128)(2,1)}, bf16[256,1024]{1,0:T(8,128)(2,1)}, u32[]{:S(2)}, u32[]{:S(2)}) collective-permute-start(bf16[256,1024]{1,0:T(8,128)(2,1)} %bitcast_convert_fusion), channel_id=1, source_target_pairs={{0,4},{4,8},{8,12},{12,16},{16,20},{20,24},{24,28},{1,5},{5,9},{9,... | collective-permute-start | bytes 1572872 | tf_op jit(solution)/shard_map/ppermute | solution.py:21
  175.1 37.1 %collective-permute-start.4 = (bf16[256,1024]{1,0:T(8,128)(2,1)}, bf16[256,1024]{1,0:T(8,128)(2,1)}, u32[]{:S(2)}, u32[]{:S(2)}) collective-permute-start(bf16[256,1024]{1,0:T(8,128)(2,1)} %bitcast_convert_fusion), channel_id=1, source_target_pairs={{4,0},{8,4},{12,8},{16,12},{20,16},{24,20},{28,24},{5,1},{9,5},{13... | collective-permute-start | bytes 1572872 | tf_op jit(solution)/shard_map/ppermute | solution.py:21
  304.5 3.2 copy-start.3
  304.5 3.1 copy-start.4
  304.6 3.1 copy-start.5
  304.6 3.1 copy-start.6
Sparse Core Ops, SparseCore 0:
  10.4 37.8 all-gather.3
  50.8 35.1 all-gather.5
  88.4 34.6 all-gather.7
  134.0 35.4 reduce-scatter.7
  172.3 35.1 reduce-scatter.3
  210.3 35.1 reduce-scatter.5
where the time goes:
time: 321 us; the launch traced here: 320 us
  waiting for transfers between devices  151 us (47%)
  matrix products  43.9 us (14%)
  between operations  36.6 us (11%)
  other arithmetic  27.2 us (8%)
  blocking collectives  24.9 us (8%)
  local copies, waits for them, and re-layouts  16 us (5%)
  starting transfers between devices  15.9 us (5%)
  loops' own time  5.35 us (2%)
    all_gather x3, waiting for transfers between devices, on_device(): lax.all_gather(for_sending(lowered), 'dp', axis=0, tiled=True)  90.8 us
    reduce_scatter x1, waiting for transfers between devices, on_device(): lax.psum_scatter(dot_tn(hid, d_resid).astype(jnp.bfloat16), 'dp', scatter...  33.3 us
    reduce_scatter x1, waiting for transfers between devices, on_device(): lax.psum_scatter(dot_tn(rows, d_pre).astype(jnp.bfloat16), 'dp', scatter_...  26.2 us
    dot_general x3, matrix products, dot_tn(): lax.dot_general(left, right, (((0,), (0,)), ((), ())), preferred_element_...  19.9 us
    ppermute x6, starting transfers between devices, passed_along(): return lax.ppermute(block, axis, route)  15.4 us
    psum x1, blocking collectives, on_device(): lax.psum(len_behind + jnp.where(index == count - 1, len_ahead, 0.0), 'cha...  14.6 us
    reduce_sum x3, other arithmetic, inner(): total = total + jnp.sum(left * right)  14 us
    psum x1, blocking collectives, on_device(): lax.psum((inner(ahead, ahead), inner(behind, behind), inner(ahead, behind...  10.2 us
  transfers between devices with their start and end apart: 12, of which 5 were waited for; matrix products, arithmetic and copies ran while one was open for 18% of the time, Pallas kernels for 0%

commit v1 on v0

v1 whole, which is shorter than its diff:
```python
import functools

import jax
import jax.numpy as jnp
from jax import lax
from jax.experimental import pallas as pl
from jax.experimental.pallas import tpu as pltpu
from jax.sharding import PartitionSpec as P

SPRING = 0.03
EPS = 1e-06
TILE = 256
LANES = 128
F32 = jnp.float32
BF16 = jnp.bfloat16


def grid_of(count):
    rows = max(k for k in range(1, count + 1) if count % k == 0 and k * k <= count)
    return rows, count // rows


def copies_of(count, chain):
    gy, gx = grid_of(count)
    gather = 2 * (gx - 1) + 2 * (gy - 1) + 2 * (gx - 1) * (gy - 1)
    scatter = (gy - 1) * gx + (gx - 1) * gy + (gx - 1) + (gy - 1)
    return 3 * (gather + scatter) + 2 * (count - 1) + (chain - 1) + 6


def dot_nn(left, right):
    return jnp.dot(left, right, preferred_element_type=F32)


def dot_nt(left, right):
    return lax.dot_general(left, right, (((1,), (1,)), ((), ())), preferred_element_type=F32)


def dot_tn(left, right):
    return lax.dot_general(left, right, (((0,), (0,)), ((), ())), preferred_element_type=F32)


def fold(value):
    part = jnp.sum(value.reshape(value.shape[0] // 8, 8, value.shape[1]), axis=0)
    total = part[:, :LANES]
    for k in range(1, value.shape[1] // LANES):
        total = total + part[:, k * LANES : (k + 1) * LANES]
    return total


def whole(tile):
    return jnp.sum(tile, axis=(0, 1), keepdims=True)


def kernel(
    n,
    c,
    classes,
    p_in,
    p_mid,
    p_out,
    e_in,
    e_mid,
    e_out,
    pool,
    picks,
    labs,
    climb,
    o_in,
    o_mid,
    o_out,
    o_energy,
    o_arc,
    o_bend,
    own,
    edge,
    thin,
    tau,
    wide,
    near,
    before,
    after,
    pool_v,
    hot,
    lab_t,
    rows,
    slope,
    hid,
    resid,
    dlog,
    dres,
    grad,
    from_y,
    from_x,
    last_x,
    last_y,
    sums,
    spans,
    late,
    load_sem,
    send_sem,
    recv_sem,
):
    ci, me = lax.axis_index("chain"), lax.axis_index("dp")
    gy, gx = grid_of(n)
    my, mx = me // gx, lax.rem(me, gx)
    block, width = own.shape[1], own.shape[2]
    depth = n * block
    half = block // 2
    step = min(32, half)
    batch = rows.shape[0]
    tiles = width // TILE
    factor = (depth**-0.5, width**-0.5, depth**-0.5)
    norm = 1.0 / (batch * n * classes)
    counter = [0]

    def remote(src, dst, to):
        k = counter[0]
        counter[0] += 1
        copy = pltpu.make_async_remote_copy(
            src_ref=src,
            dst_ref=dst,
            send_sem=send_sem.at[k],
            recv_sem=recv_sem.at[k],
            device_id=to,
            device_id_type=pl.DeviceIdType.MESH,
        )
        return copy

    def dp_peer(y, x):
        return (ci, y * gx + x)

    def y_at(d):
        return lax.rem(my + d, gy)

    def x_at(d):
        return lax.rem(mx + d, gx)

    barrier = pltpu.get_barrier_semaphore()
    for d in range(1, n):
        pl.semaphore_signal(
            barrier, inc=1, device_id=(ci, lax.rem(me + d, n)), device_id_type=pl.DeviceIdType.MESH
        )
    for d in range(1, c):
        pl.semaphore_signal(
            barrier, inc=1, device_id=(lax.rem(ci + d, c), me), device_id_type=pl.DeviceIdType.MESH
        )

    end = jnp.where(ci == 0, 0, 1)
    loads = [
        pltpu.make_async_copy(p_in.at[0], own.at[0], load_sem.at[0]),
        pltpu.make_async_copy(p_mid.at[0], own.at[1], load_sem.at[1]),
        pltpu.make_async_copy(p_out.at[0], thin.at[0], load_sem.at[2]),
        pltpu.make_async_copy(pool, pool_v, load_sem.at[3]),
        pltpu.make_async_copy(e_in.at[end], edge.at[0], load_sem.at[4]),
        pltpu.make_async_copy(e_mid.at[end], edge.at[1], load_sem.at[5]),
        pltpu.make_async_copy(e_out.at[end], thin.at[1], load_sem.at[6]),
    ]
    for load in loads:
        load.start()

    def widened(into, thin_at):
        pad = classes // LANES * LANES

        def body(r, _):
            at = pl.ds(pl.multiple_of(r * step, step), step)
            if pad < width:
                into[at, pad:] = jnp.zeros((step, width - pad), F32)
            into[at, :classes] = thin[thin_at, at, :]
            return 0

        lax.fori_loop(0, block // step, body, 0)

    def lowered(m):
        def body(r, _):
            off = pl.multiple_of(r * step, step)
            value = own[m, pl.ds(off, step), :]
            wide[m, pl.ds(pl.multiple_of(me * block + off, step), step), :] = (
                value * factor[m]
            ).astype(BF16)
            near[m, pl.ds(off, step), :] = value.astype(BF16)
            return 0

        lax.fori_loop(0, block // step, body, 0)

    for m in range(3):
        loads[m].wait()
        if m == 2:
            widened(own.at[2], 0)
        lowered(m)
    pl.semaphore_wait(barrier, n - 1 + c - 1)

    def piece(ref, m, index, h):
        return ref.at[m, pl.ds(pl.multiple_of(index * block + h * half, half), half), :]

    started = []

    def begin(copy):
        copy.start()
        started.append(copy)
        return copy

    first, own_far, second = {}, {}, {}

    def send_own(m):
        a, b = piece(wide, m, me, 0), piece(wide, m, me, 1)
        first[m] = (
            [begin(remote(a, a, dp_peer(my, x_at(d)))) for d in range(1, gx)],
            [begin(remote(b, b, dp_peer(y_at(d), mx))) for d in range(1, gy)],
        )
        own_far[m] = [begin(remote(a, a, dp_peer(y_at(d), mx))) for d in range(1, gy)] + [
            begin(remote(b, b, dp_peer(my, x_at(d)))) for d in range(1, gx)
        ]

    def forward(m):
        second[m] = []
        for d in range(1, gx):
            first[m][0][d - 1].wait_recv()
            a = piece(wide, m, my * gx + x_at(gx - d), 0)
            for e in range(1, gy):
                second[m].append(begin(remote(a, a, dp_peer(y_at(e), mx))))
        for d in range(1, gy):
            first[m][1][d - 1].wait_recv()
            b = piece(wide, m, y_at(gy - d) * gx + mx, 1)
            for e in range(1, gx):
                second[m].append(begin(remote(b, b, dp_peer(my, x_at(e)))))

    def gathered(m):
        for copy in own_far[m] + second[m]:
            copy.wait_recv()

    send_own(0)
    send_own(1)
    ups = [remote(near.at[m], before.at[m], (lax.rem(ci + 1, c), me)) for m in range(3)]
    downs = [remote(near.at[m], after.at[m], (lax.rem(ci + c - 1, c), me)) for m in range(3)]
    has_next, has_prev = ci < c - 1, ci > 0

    @pl.when(has_next)
    def _():
        for copy in ups:
            copy.start()

    @pl.when(has_prev)
    def _():
        for copy in downs:
            copy.start()

    send_own(2)

    row_of = jnp.broadcast_to(picks[...], (LANES, batch)).T
    lab_t[...] = jnp.broadcast_to(labs[...], (LANES, batch)).T
    lane = lax.broadcasted_iota(jnp.int32, (batch, LANES), 1)
    for k in range(pool_v.shape[0] // LANES):
        hot[:, k * LANES : (k + 1) * LANES] = (row_of == lane + k * LANES).astype(F32).astype(BF16)
    loads[3].wait()

    def column(t):
        return pl.ds(pl.multiple_of(t * TILE, TILE), TILE)

    @pl.loop(0, tiles)
    def _(t):
        at = column(t)
        rows[:, at] = dot_nn(hot[...], pool_v[:, at]).astype(BF16)

    forward(0)

    for load in loads[4:]:
        load.wait()
    widened(edge.at[2], 1)

    @pl.when(has_prev)
    def _():
        for copy in ups:
            copy.wait_recv()

    @pl.when(has_next)
    def _():
        for copy in downs:
            copy.wait_recv()

    def differences(m, at):
        mine = own[m, at, :]
        fixed = edge[m, at, :]
        left = jnp.where(ci == 0, fixed, before[m, at, :].astype(F32))
        right = jnp.where(ci == c - 1, fixed, after[m, at, :].astype(F32))
        return right - mine, mine - left

    zero = jnp.zeros((8, LANES), F32)

    def span_sums(m, carry):
        def body(r, carry):
            ahead, behind = differences(m, pl.ds(pl.multiple_of(r * step, step), step))
            return (
                carry[0] + fold(ahead * ahead),
                carry[1] + fold(behind * behind),
                carry[2] + fold(ahead * behind),
            )

        return lax.fori_loop(0, block // step, body, carry)

    carry = (zero, zero, zero)
    for m in range(3):
        carry = span_sums(m, carry)
    for k in range(3):
        sums[me, k] = carry[k]
    sums_out = [
        begin(remote(sums.at[me], sums.at[me], (ci, lax.rem(me + d, n)))) for d in range(1, n)
    ]

    forward(1)
    gathered(0)

    @pl.loop(0, tiles)
    def _(t):
        at = column(t)
        pre = dot_nn(rows[...], wide[0, :, at])
        sig = jax.nn.sigmoid(pre)
        hid[:, at] = (pre * sig).astype(BF16)
        slope[:, at] = sig * (1.0 + pre * (1.0 - sig))

    forward(2)

    for copy in sums_out:
        copy.wait_recv()

    def over_dp(ref, k):
        total = ref[0, k]
        for j in range(1, n):
            total = total + ref[j, k]
        return whole(total)

    sq_ahead, sq_behind, cross = (over_dp(sums, k) for k in range(3))
    len_ahead = jnp.sqrt(sq_ahead + EPS)
    len_behind = jnp.sqrt(sq_behind + EPS)
    raw_sq = (
        sq_ahead / (len_ahead * len_ahead)
        + sq_behind / (len_behind * len_behind)
        + 2.0 * cross / (len_ahead * len_behind)
    )
    raw_len = jnp.sqrt(raw_sq + EPS)
    spans[ci, 0] = jnp.broadcast_to(len_behind, (8, LANES))
    spans[ci, 1] = jnp.broadcast_to(len_ahead, (8, LANES))
    spans_out = [
        begin(remote(spans.at[ci], spans.at[ci], (lax.rem(ci + d, c), me))) for d in range(1, c)
    ]

    gathered(1)

    @pl.loop(0, tiles)
    def _(t):
        at = column(t)
        resid[:, at] = (rows[:, at].astype(F32) + dot_nn(hid[...], wide[1, :, at])).astype(BF16)

    gathered(2)

    def classify(t, energy):
        at = column(t)
        logits = dot_nn(resid[...], wide[2, :, at])
        parts = []
        for k in range(TILE // LANES):
            target = (lab_t[...] == lane + (t * TILE + k * LANES)).astype(F32)
            err = logits[:, k * LANES : (k + 1) * LANES] - target
            energy = energy + fold(err * err)
            parts.append((err * norm).astype(BF16))
        dlog[:, at] = jnp.concatenate(parts, axis=1)
        return energy

    energy = lax.fori_loop(0, tiles, classify, zero)

    def products(m, left, right):
        @pl.loop(0, depth // TILE)
        def _(t):
            at = column(t)
            grad[m, at, :] = dot_tn(left[:, at], right[...]).astype(BF16)

    to_rows, to_cols, back_x, back_y = {}, {}, {}, {}

    def scatter(m):
        to_rows[m], to_cols[m] = [], []
        for d in range(1, gy):
            for x in range(gx):
                to_rows[m].append(
                    begin(
                        remote(
                            piece(grad, m, y_at(d) * gx + x, 0),
                            from_y.at[m, d - 1, x],
                            dp_peer(y_at(d), mx),
                        )
                    )
                )
        for d in range(1, gx):
            for y in range(gy):
                to_cols[m].append(
                    begin(
                        remote(
                            piece(grad, m, y * gx + x_at(d), 1),
                            from_x.at[m, d - 1, y],
                            dp_peer(my, x_at(d)),
                        )
                    )
                )

    def combine(m, index, h, arrived, count, slot):
        def body(r, _):
            off = pl.multiple_of(r * step, step)
            at = pl.ds(pl.multiple_of(index * block + h * half + off, step), step)
            total = grad[m, at, :].astype(F32)
            for d in range(count):
                total = total + arrived[m, d, slot, pl.ds(off, step), :].astype(F32)
            grad[m, at, :] = total.astype(BF16)
            return 0

        lax.fori_loop(0, half // step, body, 0)

    def scatter_on(m):
        for copy in to_rows[m]:
            copy.wait_recv()
        back_x[m] = []
        for d in range(1, gx):
            index = my * gx + x_at(d)
            combine(m, index, 0, from_y, gy - 1, x_at(d))
            back_x[m].append(
                begin(remote(piece(grad, m, index, 0), last_x.at[m, d - 1], dp_peer(my, x_at(d))))
            )
        for copy in to_cols[m]:
            copy.wait_recv()
        back_y[m] = []
        for d in range(1, gy):
            index = y_at(d) * gx + mx
            combine(m, index, 1, from_x, gx - 1, y_at(d))
            back_y[m].append(
                begin(remote(piece(grad, m, index, 1), last_y.at[m, d - 1], dp_peer(y_at(d), mx)))
            )

    products(2, resid, dlog)
    scatter(2)

    @pl.loop(0, depth // TILE)
    def _(t):
        at = column(t)
        dres[:, at] = dot_nt(dlog[...], wide[2, at, :]).astype(BF16)

    products(1, hid, dres)
    scatter(1)

    @pl.loop(0, depth // TILE)
    def _(t):
        at = column(t)
        dlog[:, at] = (dot_nt(dres[...], wide[1, at, :]) * slope[:, at]).astype(BF16)

    products(0, rows, dlog)
    scatter(0)

    for copy in spans_out:
        copy.wait_recv()
    by_ahead = 1.0 / (len_ahead * raw_len)
    by_behind = 1.0 / (len_behind * raw_len)

    for m in range(3):

        def body(r, _, m=m):
            at = pl.ds(pl.multiple_of(r * step, step), step)
            ahead, behind = differences(m, at)
            tau[m, at, :] = ahead * by_ahead + behind * by_behind
            return 0

        lax.fori_loop(0, block // step, body, 0)

    arc = jnp.zeros((1, 1), F32)
    band = jnp.zeros((1, 1), F32)
    for k in range(c):
        length = spans[k, 0, 0:1, 0:1]
        arc = arc + jnp.where(k <= ci, length, 0.0)
        band = band + length
    band = band + spans[c - 1, 1, 0:1, 0:1]

    for m in (2, 1, 0):
        scatter_on(m)

    def finish(m, carry):
        for copy in back_x[m] + back_y[m]:
            copy.wait_recv()
        for h, arrived, count, slot, last, lasts in (
            (0, from_y, gy - 1, mx, last_x, gx - 1),
            (1, from_x, gx - 1, my, last_y, gy - 1),
        ):

            def body(r, carry):
                off = pl.multiple_of(r * step, step)
                total = grad[
                    m, pl.ds(pl.multiple_of(me * block + h * half + off, step), step), :
                ].astype(F32)
                for d in range(count):
                    total = total + arrived[m, d, slot, pl.ds(off, step), :].astype(F32)
                for d in range(lasts):
                    total = total + last[m, d, pl.ds(off, step), :].astype(F32)
                total = total * factor[m]
                at = pl.ds(h * half + off, step)
                edge[m, at, :] = total
                return carry[0] + fold(total * tau[m, at, :]), carry[1] + fold(total * total)

            carry = lax.fori_loop(0, half // step, body, carry)
        return carry

    carry = (zero, zero)
    for m in (2, 1, 0):
        carry = finish(m, carry)
    late[me, 0] = carry[0]
    late[me, 1] = carry[1]
    late[me, 2] = energy * (0.5 * norm)
    late_out = [
        begin(remote(late.at[me], late.at[me], (ci, lax.rem(me + d, n)))) for d in range(1, n)
    ]
    for copy in late_out:
        copy.wait_recv()
    along, g_g, energy_all = (over_dp(late, k) for k in range(3))

    goal = (ci + 1).astype(F32) / (c + 1) * band
    coef = jnp.where(climb[...] == 1, 2.0 * along, along + SPRING * (goal - arc) / band)
    tau_sq = raw_sq / (raw_sq + EPS)
    force_sq = g_g - 2.0 * coef * along + coef * coef * tau_sq
    scale = band / (c + 1) / jnp.sqrt(force_sq + EPS)
    push = scale * coef
    o_energy[...] = energy_all
    o_arc[...] = arc / band
    o_bend[...] = 0.5 * raw_len

    stores = []
    for m, out in ((2, o_out), (1, o_mid), (0, o_in)):

        def body(r, _, m=m):
            at = pl.ds(pl.multiple_of(r * step, step), step)
            new = own[m, at, :] + (push * tau[m, at, :] - scale * edge[m, at, :])
            if m == 2:
                thin[0, at, :] = new[:, :classes]
            else:
                tau[m, at, :] = new
            return 0

        lax.fori_loop(0, block // step, body, 0)
        copy = pltpu.make_async_copy(
            thin.at[0] if m == 2 else tau.at[m], out.at[0], load_sem.at[m]
        )
        copy.start()
        stores.append(copy)

    @pl.when(has_next)
    def _():
        for copy in ups:
            copy.wait_send()

    @pl.when(has_prev)
    def _():
        for copy in downs:
            copy.wait_send()

    for copy in started:
        copy.wait_send()
    for copy in stores:
        copy.wait()


def on_device(
    n,
    c,
    images_in,
    images_mid,
    images_out,
    ends_in,
    ends_mid,
    ends_out,
    data_pool,
    batch_rows,
    labels,
    climbing,
):
    block, width = images_in.shape[1], images_in.shape[2]
    classes = images_out.shape[2]
    depth = n * block
    half = block // 2
    batch = batch_rows.shape[1]
    gy, gx = grid_of(n)
    copies = copies_of(n, c)
    vmem = pl.BlockSpec(memory_space=pltpu.VMEM)
    anywhere = pl.BlockSpec(memory_space=pl.ANY)
    small = jax.ShapeDtypeStruct((1, 1), F32)
    outs = pl.pallas_call(
        functools.partial(kernel, n, c, classes),
        out_shape=(
            jax.ShapeDtypeStruct(images_in.shape, F32),
            jax.ShapeDtypeStruct(images_mid.shape, F32),
            jax.ShapeDtypeStruct(images_out.shape, F32),
            small,
            small,
            small,
        ),
        in_specs=[anywhere] * 7 + [vmem] * 3,
        out_specs=[anywhere] * 3 + [vmem] * 3,
        scratch_shapes=[
            pltpu.VMEM((3, block, width), F32),
            pltpu.VMEM((3, block, width), F32),
            pltpu.VMEM((2, block, classes), F32),
            pltpu.VMEM((3, block, width), F32),
            pltpu.VMEM((3, depth, width), BF16),
            pltpu.VMEM((3, block, width), BF16),
            pltpu.VMEM((3, block, width), BF16),
            pltpu.VMEM((3, block, width), BF16),
            pltpu.VMEM(data_pool.shape, BF16),
            pltpu.VMEM((batch, data_pool.shape[0]), BF16),
            pltpu.VMEM((batch, LANES), jnp.int32),
            pltpu.VMEM((batch, depth), BF16),
            pltpu.VMEM((batch, width), F32),
            pltpu.VMEM((batch, width), BF16),
            pltpu.VMEM((batch, depth), BF16),
            pltpu.VMEM((batch, width), BF16),
            pltpu.VMEM((batch, depth), BF16),
            pltpu.VMEM((3, depth, width), BF16),
            pltpu.VMEM((3, max(gy - 1, 1), gx, half, width), BF16),
            pltpu.VMEM((3, max(gx - 1, 1), gy, half, width), BF16),
            pltpu.VMEM((3, max(gx - 1, 1), half, width), BF16),
            pltpu.VMEM((3, max(gy - 1, 1), half, width), BF16),
            pltpu.VMEM((n, 3, 8, LANES), F32),
            pltpu.VMEM((c, 2, 8, LANES), F32),
            pltpu.VMEM((n, 3, 8, LANES), F32),
            pltpu.SemaphoreType.DMA((7,)),
            pltpu.SemaphoreType.DMA((copies,)),
            pltpu.SemaphoreType.DMA((copies,)),
        ],
        compiler_params=pltpu.CompilerParams(
            collective_id=0, has_side_effects=True, vmem_limit_bytes=63 * 1024 * 1024
        ),
    )(
        images_in,
        images_mid,
        images_out,
        ends_in,
        ends_mid,
        ends_out,
        data_pool,
        batch_rows,
        labels,
        climbing[:, None],
    )
    return (*outs[:3], outs[3][0], outs[4][0], outs[5][0])


def solution(mesh):
    placed = (
        P("chain", "dp", None),
        P("chain", "dp", None),
        P("chain", "dp", None),
        P(None, "dp", None),
        P(None, "dp", None),
        P(None, "dp", None),
        P("dp", None),
        P("chain", "dp"),
        P("chain", "dp"),
        P("chain"),
    )
    return jax.shard_map(
        functools.partial(on_device, mesh.shape["dp"], mesh.shape["chain"]),
        mesh=mesh,
        in_specs=placed,
        out_specs=(
            P("chain", "dp", None),
            P("chain", "dp", None),
            P("chain", "dp", None),
            P("chain"),
            P("chain"),
            P("chain"),
        ),
        check_vma=False,
    )
```

time: 321 us -> 142 us (0.44)
  waiting for transfers between devices: 151 us -> 0 us
  Pallas kernels: 0 us -> 125 us
  matrix products: 43.9 us -> 0 us
  between operations: 36.6 us -> 6.63 us
  other arithmetic: 27.2 us -> 0 us
  blocking collectives: 24.9 us -> 0 us
  starting transfers between devices: 15.9 us -> 0 us
  local copies, waits for them, and re-layouts: 16 us -> 10.3 us
  loops' own time: 5.35 us -> 0 us
    pallas_call x0 -> x1, Pallas kernels: none -> 125 us  [on_device(): pl.pallas_call(functools.partial(kernel, n, c, classes), out_shape=(jax.S...]
    all_gather x3 -> x0, waiting for transfers between devices: 90.8 us -> none  [on_device(): lax.all_gather(for_sending(lowered), 'dp', axis=0, tiled=True)]
    reduce_scatter x3 -> x0, waiting for transfers between devices: 59.6 us -> none  [the longest x1 33.3 us: on_device(): lax.psum_scatter(dot_tn(hid, d_resid).astype(jnp.bfloat16), 'dp', scatter...]
    dot_general x7 -> x0, matrix products: 43.9 us -> none  [the longest x3 19.9 us: dot_tn(): lax.dot_general(left, right, (((0,), (0,)), ((), ())), preferred_element_...]
    psum x2 -> x0, blocking collectives: 24.9 us -> none  [the longest x1 14.6 us: on_device(): lax.psum(len_behind + jnp.where(index == count - 1, len_ahead, 0.0), 'cha...]
    ppermute x6 -> x0, starting transfers between devices: 15.4 us -> none  [passed_along(): return lax.ppermute(block, axis, route)]
    reduce_sum x3 -> x0, other arithmetic: 14 us -> none  [inner(): total = total + jnp.sum(left * right)]
    gather x1 -> x0, local copies, waits for them, and re-layouts: 8.05 us -> none  [on_device(): rows = data_pool[batch_rows[0]]]
  transfers between devices with their start and end apart: 12 -> 0, of which waited for: 5 -> 0; matrix products, arithmetic and copies ran while one was open for 18% -> 0% of each run, Pallas kernels for 0% -> 0%
where the time goes in v1:
time: 142 us
  Pallas kernels  125 us (88%)
  local copies, waits for them, and re-layouts  10.3 us (7%)
  between operations  6.63 us (5%)
    pallas_call x1, Pallas kernels, on_device(): pl.pallas_call(functools.partial(kernel, n, c, classes), out_shape=(jax.S...  125 us
    unnamed x9, local copies, waits for them, and re-layouts  10.3 us

profile of v1, /device:TPU:0, one launch (start us, length us, event | category | flops | bytes accessed | tf_op | source)
XLA Modules:
  0.0 141.7 jit_solution(3742044505659320620)
XLA Ops:
  0.6 0.0 copy-start
  1.4 2.5 %copy.16.p_out = f32[1,256,1000]{2,1,0:T(8,128)} copy(f32[1,256,1000]{1,2,0:T(8,128)} %param.12) | data formatting | bytes 2048000 | tf_op args[2]
  4.0 0.0 copy-done
  4.0 1.9 %copy.17.e_out = f32[2,256,1000]{2,1,0:T(8,128)} copy(f32[2,256,1000]{1,2,0:T(8,128)S(1)} %copy-done) | data formatting | bytes 4096000 | tf_op args[5]
  5.8 124.9 %shard_map.145 = (f32[1,256,1024]{2,1,0:T(8,128)}, f32[1,256,1024]{2,1,0:T(8,128)}, f32[1,256,1000]{2,1,0:T(8,128)}, f32[1,1]{1,0:T(1,128)}, f32[1,1]{1,0:T(1,128)}, /*index=5*/f32[1,1]{1,0:T(1,128)}) custom-call(f32[1,256,1024]{2,1,0:T(8,128)} %p_in.1, f32[1,256,1024]{2,1,0:T(8,128)} %p_mid.1, f32[1,256,1000]{2,1,0:T(8,128)} %copy.16.p_out, ...), custom_call_target="tpu_custom_call" | custom-call | tf_op jit(solution)/shard_map/pallas_call | solution.py:586
  130.7 0.0 copy-start.1
  130.7 2.6 %copy.18 = f32[1,256,1000]{1,2,0:T(8,128)} copy(f32[1,256,1000]{2,1,0:T(8,128)} %get-tuple-element.20) | data formatting | bytes 2048000
  133.3 2.3 %copy.25 = f32[1,256,1024]{2,1,0:T(8,128)} copy(f32[1,256,1024]{2,1,0:T(8,128)} %get-tuple-element.30) | data formatting | bytes 2097152
  135.6 0.0 copy-done.1
  135.6 1.0 copy.26
Async XLA Ops:
  0.6 3.3 %copy-start = (f32[2,256,1000]{1,2,0:T(8,128)S(1)}, f32[2,256,1000]{1,2,0:T(8,128)}, u32[]{:S(2)}) copy-start(f32[2,256,1000]{1,2,0:T(8,128)} %param.15) | copy-start | bytes 6144004
  130.7 4.9 %copy-start.1 = (f32[1,256,1024]{2,1,0:T(8,128)S(1)}, f32[1,256,1024]{2,1,0:T(8,128)}, u32[]{:S(2)}) copy-start(f32[1,256,1024]{2,1,0:T(8,128)} %get-tuple-element.31) | copy-start | bytes 3145732

commit v2 on v1

--- a/solution.py
+++ b/solution.py
@@ -20,11 +20,12 @@
     return rows, count // rows
 
 
-def copies_of(count, chain):
+def copies_of(count, chain, chunks):
     gy, gx = grid_of(count)
     gather = 2 * (gx - 1) + 2 * (gy - 1) + 2 * (gx - 1) * (gy - 1)
-    scatter = (gy - 1) * gx + (gx - 1) * gy + (gx - 1) + (gy - 1)
-    return 3 * (gather + scatter) + 2 * (count - 1) + (chain - 1) + 6
+    scatter = (gy - 1) * gx + (gx - 1) * gy
+    back = (gx - 1) + (gy - 1)
+    return (2 + chunks) * (gather + scatter) + 3 * back + 2 * (count - 1) + (chain - 1) + 6
 
 
 def dot_nn(left, right):
@@ -86,6 +87,9 @@
     slope,
     hid,
     resid,
+    rows_t,
+    hid_t,
+    resid_t,
     dlog,
     dres,
     grad,
@@ -149,26 +153,26 @@
     loads = [
         pltpu.make_async_copy(p_in.at[0], own.at[0], load_sem.at[0]),
         pltpu.make_async_copy(p_mid.at[0], own.at[1], load_sem.at[1]),
-        pltpu.make_async_copy(p_out.at[0], thin.at[0], load_sem.at[2]),
+        pltpu.make_async_copy(p_out.at[0], thin.at[0, pl.ds(0, classes)], load_sem.at[2]),
         pltpu.make_async_copy(pool, pool_v, load_sem.at[3]),
         pltpu.make_async_copy(e_in.at[end], edge.at[0], load_sem.at[4]),
         pltpu.make_async_copy(e_mid.at[end], edge.at[1], load_sem.at[5]),
-        pltpu.make_async_copy(e_out.at[end], thin.at[1], load_sem.at[6]),
+        pltpu.make_async_copy(e_out.at[end], thin.at[1, pl.ds(0, classes)], load_sem.at[6]),
     ]
     for load in loads:
         load.start()
 
-    def widened(into, thin_at):
-        pad = classes // LANES * LANES
-
-        def body(r, _):
-            at = pl.ds(pl.multiple_of(r * step, step), step)
-            if pad < width:
-                into[at, pad:] = jnp.zeros((step, width - pad), F32)
-            into[at, :classes] = thin[thin_at, at, :]
-            return 0
-
-        lax.fori_loop(0, block // step, body, 0)
+    def turned(into, thin_at):
+        @pl.loop(0, width // LANES)
+        def _(k):
+            at = pl.ds(pl.multiple_of(k * LANES, LANES), LANES)
+            into[:, at] = thin[thin_at, at, :].T
+
+    def blanked(thin_at):
+        if classes < width:
+            thin[thin_at, pl.ds(classes, width - classes), :] = jnp.zeros(
+                (width - classes, block), F32
+            )
 
     def lowered(m):
         def body(r, _):
@@ -182,15 +186,20 @@
 
         lax.fori_loop(0, block // step, body, 0)
 
-    for m in range(3):
+    for m in range(2):
         loads[m].wait()
-        if m == 2:
-            widened(own.at[2], 0)
         lowered(m)
+    blanked(0)
+    blanked(1)
     pl.semaphore_wait(barrier, n - 1 + c - 1)
 
-    def piece(ref, m, index, h):
-        return ref.at[m, pl.ds(pl.multiple_of(index * block + h * half, half), half), :]
+    def column(t):
+        return pl.ds(pl.multiple_of(t * TILE, TILE), TILE)
+
+    everything = pl.ds(0, width)
+
+    def piece(ref, m, index, h, at=everything):
+        return ref.at[m, pl.ds(pl.multiple_of(index * block + h * half, half), half), at]
 
     started = []
 
@@ -201,35 +210,46 @@
 
     first, own_far, second = {}, {}, {}
 
-    def send_own(m):
-        a, b = piece(wide, m, me, 0), piece(wide, m, me, 1)
-        first[m] = (
+    def send_own(key, m, at=everything):
+        a, b = piece(wide, m, me, 0, at), piece(wide, m, me, 1, at)
+        first[key] = (
             [begin(remote(a, a, dp_peer(my, x_at(d)))) for d in range(1, gx)],
             [begin(remote(b, b, dp_peer(y_at(d), mx))) for d in range(1, gy)],
         )
-        own_far[m] = [begin(remote(a, a, dp_peer(y_at(d), mx))) for d in range(1, gy)] + [
+        own_far[key] = [begin(remote(a, a, dp_peer(y_at(d), mx))) for d in range(1, gy)] + [
             begin(remote(b, b, dp_peer(my, x_at(d)))) for d in range(1, gx)
         ]
 
-    def forward(m):
-        second[m] = []
+    def forward(key, m, at=everything):
+        second[key] = []
         for d in range(1, gx):
-            first[m][0][d - 1].wait_recv()
-            a = piece(wide, m, my * gx + x_at(gx - d), 0)
+            first[key][0][d - 1].wait_recv()
+            a = piece(wide, m, my * gx + x_at(gx - d), 0, at)
             for e in range(1, gy):
-                second[m].append(begin(remote(a, a, dp_peer(y_at(e), mx))))
+                second[key].append(begin(remote(a, a, dp_peer(y_at(e), mx))))
         for d in range(1, gy):
-            first[m][1][d - 1].wait_recv()
-            b = piece(wide, m, y_at(gy - d) * gx + mx, 1)
+            first[key][1][d - 1].wait_recv()
+            b = piece(wide, m, y_at(gy - d) * gx + mx, 1, at)
             for e in range(1, gx):
-                second[m].append(begin(remote(b, b, dp_peer(my, x_at(e)))))
-
-    def gathered(m):
-        for copy in own_far[m] + second[m]:
+                second[key].append(begin(remote(b, b, dp_peer(my, x_at(e)))))
+
+    def gathered(key):
+        for copy in own_far[key] + second[key]:
             copy.wait_recv()
 
-    send_own(0)
-    send_own(1)
+    def send_chunk(t):
+        if t < tiles:
+            send_own((2, t), 2, pl.ds(t * TILE, TILE))
+
+    def forward_chunk(t):
+        if t < tiles:
+            forward((2, t), 2, pl.ds(t * TILE, TILE))
+
+    send_own(0, 0)
+    send_own(1, 1)
+    loads[2].wait()
+    turned(own.at[2], 0)
+    lowered(2)
     ups = [remote(near.at[m], before.at[m], (lax.rem(ci + 1, c), me)) for m in range(3)]
     downs = [remote(near.at[m], after.at[m], (lax.rem(ci + c - 1, c), me)) for m in range(3)]
     has_next, has_prev = ci < c - 1, ci > 0
@@ -243,8 +263,6 @@
     def _():
         for copy in downs:
             copy.start()
-
-    send_own(2)
 
     row_of = jnp.broadcast_to(picks[...], (LANES, batch)).T
     lab_t[...] = jnp.broadcast_to(labs[...], (LANES, batch)).T
@@ -253,19 +271,19 @@
         hot[:, k * LANES : (k + 1) * LANES] = (row_of == lane + k * LANES).astype(F32).astype(BF16)
     loads[3].wait()
 
-    def column(t):
-        return pl.ds(pl.multiple_of(t * TILE, TILE), TILE)
-
     @pl.loop(0, tiles)
     def _(t):
         at = column(t)
-        rows[:, at] = dot_nn(hot[...], pool_v[:, at]).astype(BF16)
-
-    forward(0)
+        picked = dot_nn(hot[...], pool_v[:, at]).astype(BF16)
+        rows[:, at] = picked
+        rows_t[at, :] = picked.T
+
+    forward(0, 0)
+    send_chunk(0)
 
     for load in loads[4:]:
         load.wait()
-    widened(edge.at[2], 1)
+    turned(edge.at[2], 1)
 
     @pl.when(has_prev)
     def _():
@@ -306,7 +324,8 @@
         begin(remote(sums.at[me], sums.at[me], (ci, lax.rem(me + d, n)))) for d in range(1, n)
     ]
 
-    forward(1)
+    forward(1, 1)
+    send_chunk(1)
     gathered(0)
 
     @pl.loop(0, tiles)
@@ -314,10 +333,13 @@
         at = column(t)
         pre = dot_nn(rows[...], wide[0, :, at])
         sig = jax.nn.sigmoid(pre)
-        hid[:, at] = (pre * sig).astype(BF16)
+        value = (pre * sig).astype(BF16)
+        hid[:, at] = value
+        hid_t[at, :] = value.T
         slope[:, at] = sig * (1.0 + pre * (1.0 - sig))
 
-    forward(2)
+    forward_chunk(0)
+    send_chunk(2)
 
     for copy in sums_out:
         copy.wait_recv()
@@ -348,9 +370,12 @@
     @pl.loop(0, tiles)
     def _(t):
         at = column(t)
-        resid[:, at] = (rows[:, at].astype(F32) + dot_nn(hid[...], wide[1, :, at])).astype(BF16)
-
-    gathered(2)
+        value = (rows[:, at].astype(F32) + dot_nn(hid[...], wide[1, :, at])).astype(BF16)
+        resid[:, at] = value
+        resid_t[at, :] = value.T
+
+    forward_chunk(1)
+    send_chunk(3)
 
     def classify(t, energy):
         at = column(t)
@@ -364,25 +389,24 @@
         dlog[:, at] = jnp.concatenate(parts, axis=1)
         return energy
 
-    energy = lax.fori_loop(0, tiles, classify, zero)
-
-    def products(m, left, right):
+    def products(m, left_t, right):
         @pl.loop(0, depth // TILE)
         def _(t):
             at = column(t)
-            grad[m, at, :] = dot_tn(left[:, at], right[...]).astype(BF16)
+            grad[m, at, :] = dot_nn(left_t[at, :], right[...]).astype(BF16)
 
     to_rows, to_cols, back_x, back_y = {}, {}, {}, {}
 
-    def scatter(m):
-        to_rows[m], to_cols[m] = [], []
+    def scatter(m, at=everything):
+        to_rows.setdefault(m, [])
+        to_cols.setdefault(m, [])
         for d in range(1, gy):
             for x in range(gx):
                 to_rows[m].append(
                     begin(
                         remote(
-                            piece(grad, m, y_at(d) * gx + x, 0),
-                            from_y.at[m, d - 1, x],
+                            piece(grad, m, y_at(d) * gx + x, 0, at),
+                            from_y.at[m, d - 1, x, :, at],
                             dp_peer(y_at(d), mx),
                         )
                     )
@@ -392,8 +416,8 @@
                 to_cols[m].append(
                     begin(
                         remote(
-                            piece(grad, m, y * gx + x_at(d), 1),
-                            from_x.at[m, d - 1, y],
+                            piece(grad, m, y * gx + x_at(d), 1, at),
+                            from_x.at[m, d - 1, y, :, at],
                             dp_peer(my, x_at(d)),
                         )
                     )
@@ -431,15 +455,27 @@
                 begin(remote(piece(grad, m, index, 1), last_y.at[m, d - 1], dp_peer(y_at(d), mx)))
             )
 
-    products(2, resid, dlog)
-    scatter(2)
+    energy = zero
+    for t in range(tiles):
+        gathered((2, t))
+        energy = classify(t, energy)
+        at = pl.ds(t * TILE, TILE)
+
+        @pl.loop(0, depth // TILE)
+        def _(r):
+            of = column(r)
+            grad[2, of, at] = dot_nn(resid_t[of, :], dlog[:, at]).astype(BF16)
+
+        forward_chunk(t + 2)
+        send_chunk(t + 4)
+        scatter(2, at)
 
     @pl.loop(0, depth // TILE)
     def _(t):
         at = column(t)
         dres[:, at] = dot_nt(dlog[...], wide[2, at, :]).astype(BF16)
 
-    products(1, hid, dres)
+    products(1, hid_t, dres)
     scatter(1)
 
     @pl.loop(0, depth // TILE)
@@ -447,7 +483,7 @@
         at = column(t)
         dlog[:, at] = (dot_nt(dres[...], wide[1, at, :]) * slope[:, at]).astype(BF16)
 
-    products(0, rows, dlog)
+    products(0, rows_t, dlog)
     scatter(0)
 
     for copy in spans_out:
@@ -515,31 +551,35 @@
     along, g_g, energy_all = (over_dp(late, k) for k in range(3))
 
     goal = (ci + 1).astype(F32) / (c + 1) * band
-    coef = jnp.where(climb[...] == 1, 2.0 * along, along + SPRING * (goal - arc) / band)
+    coef = jnp.where(jnp.full((1, 1), climb[0]) == 1, 2.0 * along, along + SPRING * (goal - arc) / band)
     tau_sq = raw_sq / (raw_sq + EPS)
     force_sq = g_g - 2.0 * coef * along + coef * coef * tau_sq
     scale = band / (c + 1) / jnp.sqrt(force_sq + EPS)
     push = scale * coef
-    o_energy[...] = energy_all
-    o_arc[...] = arc / band
-    o_bend[...] = 0.5 * raw_len
+    o_energy[0] = energy_all[0, 0]
+    o_arc[0] = (arc / band)[0, 0]
+    o_bend[0] = (0.5 * raw_len)[0, 0]
 
     stores = []
     for m, out in ((2, o_out), (1, o_mid), (0, o_in)):
-
-        def body(r, _, m=m):
-            at = pl.ds(pl.multiple_of(r * step, step), step)
-            new = own[m, at, :] + (push * tau[m, at, :] - scale * edge[m, at, :])
-            if m == 2:
-                thin[0, at, :] = new[:, :classes]
-            else:
-                tau[m, at, :] = new
-            return 0
-
-        lax.fori_loop(0, block // step, body, 0)
-        copy = pltpu.make_async_copy(
-            thin.at[0] if m == 2 else tau.at[m], out.at[0], load_sem.at[m]
-        )
+        if m == 2:
+
+            @pl.loop(0, width // LANES)
+            def _(k):
+                at = pl.ds(pl.multiple_of(k * LANES, LANES), LANES)
+                new = own[2, :, at] + (push * tau[2, :, at] - scale * edge[2, :, at])
+                thin[0, at, :] = new.T
+
+            source = thin.at[0, pl.ds(0, classes)]
+        else:
+
+            @pl.loop(0, block // step)
+            def _(r):
+                at = pl.ds(pl.multiple_of(r * step, step), step)
+                tau[m, at, :] = own[m, at, :] + (push * tau[m, at, :] - scale * edge[m, at, :])
+
+            source = tau.at[m]
+        copy = pltpu.make_async_copy(source, out.at[0], load_sem.at[m])
         copy.start()
         stores.append(copy)
 
@@ -579,26 +619,27 @@
     half = block // 2
     batch = batch_rows.shape[1]
     gy, gx = grid_of(n)
-    copies = copies_of(n, c)
+    copies = copies_of(n, c, width // TILE)
     vmem = pl.BlockSpec(memory_space=pltpu.VMEM)
     anywhere = pl.BlockSpec(memory_space=pl.ANY)
-    small = jax.ShapeDtypeStruct((1, 1), F32)
+    scalar = pl.BlockSpec(memory_space=pltpu.SMEM)
+    small = jax.ShapeDtypeStruct((1,), F32)
     outs = pl.pallas_call(
         functools.partial(kernel, n, c, classes),
         out_shape=(
             jax.ShapeDtypeStruct(images_in.shape, F32),
             jax.ShapeDtypeStruct(images_mid.shape, F32),
-            jax.ShapeDtypeStruct(images_out.shape, F32),
+            jax.ShapeDtypeStruct((1, classes, block), F32),
             small,
             small,
             small,
         ),
-        in_specs=[anywhere] * 7 + [vmem] * 3,
-        out_specs=[anywhere] * 3 + [vmem] * 3,
+        in_specs=[anywhere] * 7 + [vmem] * 2 + [scalar],
+        out_specs=[anywhere] * 3 + [scalar] * 3,
         scratch_shapes=[
             pltpu.VMEM((3, block, width), F32),
             pltpu.VMEM((3, block, width), F32),
-            pltpu.VMEM((2, block, classes), F32),
+            pltpu.VMEM((2, width, block), F32),
             pltpu.VMEM((3, block, width), F32),
             pltpu.VMEM((3, depth, width), BF16),
             pltpu.VMEM((3, block, width), BF16),
@@ -611,6 +652,9 @@
             pltpu.VMEM((batch, width), F32),
             pltpu.VMEM((batch, width), BF16),
             pltpu.VMEM((batch, depth), BF16),
+            pltpu.VMEM((depth, batch), BF16),
+            pltpu.VMEM((width, batch), BF16),
+            pltpu.VMEM((depth, batch), BF16),
             pltpu.VMEM((batch, width), BF16),
             pltpu.VMEM((batch, depth), BF16),
             pltpu.VMEM((3, depth, width), BF16),
@@ -631,16 +675,16 @@
     )(
         images_in,
         images_mid,
-        images_out,
+        jnp.swapaxes(images_out, 1, 2),
         ends_in,
         ends_mid,
-        ends_out,
+        jnp.swapaxes(ends_out, 1, 2),
         data_pool,
         batch_rows,
         labels,
-        climbing[:, None],
+        climbing,
     )
-    return (*outs[:3], outs[3][0], outs[4][0], outs[5][0])
+    return (outs[0], outs[1], jnp.swapaxes(outs[2], 1, 2), *outs[3:])
 
 
 def solution(mesh):

time: 142 us -> 131 us (0.923)
  Pallas kernels: 125 us -> 119 us
  local copies, waits for them, and re-layouts: 10.3 us -> 4.39 us
    unnamed x9 -> x7, local copies, waits for them, and re-layouts: 10.3 us -> 4.39 us
    pallas_call x1, Pallas kernels: 125 us -> 119 us  [on_device(): pl.pallas_call(functools.partial(kernel, n, c, classes), out_shape=(jax.S...]
where the time goes in v2:
time: 131 us; the launch traced here: 130 us
  Pallas kernels  119 us (91%)
  between operations  6.5 us (5%)
  local copies, waits for them, and re-layouts  4.39 us (3%)
    pallas_call x1, Pallas kernels, on_device(): pl.pallas_call(functools.partial(kernel, n, c, classes), out_shape=(jax.S...  119 us
    unnamed x7, local copies, waits for them, and re-layouts  4.39 us

profile of v2, /device:TPU:0, one launch (start us, length us, event | category | flops | bytes accessed | tf_op | source)
XLA Modules:
  0.0 130.4 jit_solution(5467685638467416387)
XLA Ops:
  1.3 119.5 %shard_map.145 = (f32[1,256,1024]{2,1,0:T(8,128)}, f32[1,256,1024]{2,1,0:T(8,128)}, f32[1,1000,256]{2,1,0:T(8,128)}, f32[1]{0:T(128)}, f32[1]{0:T(128)}, /*index=5*/f32[1]{0:T(128)}) custom-call(f32[1,256,1024]{2,1,0:T(8,128)} %p_in.1, f32[1,256,1024]{2,1,0:T(8,128)} %p_mid.1, f32[1,1000,256]{2,1,0:T(8,128)} %bitcast.4, f32[2,256,1024]{2,1,0:T(8,128)} %e_in.1, ...), custom_call_target="tpu_custom_call" | custom-call | tf_op jit(solution)/shard_map/pallas_call | solution.py:627
  120.7 0.0 copy-start
  120.8 0.0 copy-start.1
  120.8 2.5 %copy.23 = f32[1,256,1024]{2,1,0:T(8,128)} copy(f32[1,256,1024]{2,1,0:T(8,128)} %get-tuple-element.24) | data formatting | bytes 2097152
  123.2 0.0 copy-done
  123.2 1.0 copy.24
  124.2 0.0 copy-done.1
  124.2 1.0 copy.25
Async XLA Ops:
  120.7 2.5 %copy-start = (f32[1,256,1024]{2,1,0:T(8,128)S(1)}, f32[1,256,1024]{2,1,0:T(8,128)}, u32[]{:S(2)}) copy-start(f32[1,256,1024]{2,1,0:T(8,128)} %get-tuple-element.25) | copy-start | bytes 3145732
  120.8 3.4 %copy-start.1 = (f32[1,1000,256]{2,1,0:T(8,128)S(1)}, f32[1,1000,256]{2,1,0:T(8,128)}, u32[]{:S(2)}) copy-start(f32[1,1000,256]{2,1,0:T(8,128)} %get-tuple-element.14) | copy-start | bytes 3072004

commit v3 on v2

--- a/solution.py
+++ b/solution.py
@@ -15,17 +15,11 @@
 BF16 = jnp.bfloat16
 
 
-def grid_of(count):
-    rows = max(k for k in range(1, count + 1) if count % k == 0 and k * k <= count)
-    return rows, count // rows
-
-
 def copies_of(count, chain, chunks):
-    gy, gx = grid_of(count)
-    gather = 2 * (gx - 1) + 2 * (gy - 1) + 2 * (gx - 1) * (gy - 1)
-    scatter = (gy - 1) * gx + (gx - 1) * gy
-    back = (gx - 1) + (gy - 1)
-    return (2 + chunks) * (gather + scatter) + 3 * back + 2 * (count - 1) + (chain - 1) + 6
+    pairs = count // 2
+    gather = 1 + (pairs - 1) + pairs
+    scatter = pairs
+    return (2 + chunks) * (gather + scatter) + 3 * pairs + 2 * (count - 1) + (chain - 1) + 9
 
 
 def dot_nn(left, right):
@@ -77,12 +71,16 @@
     thin,
     tau,
     wide,
+    stage,
     near,
     before,
     after,
     pool_v,
     hot,
     lab_t,
+    lab_out,
+    lab_in,
+    rows_out,
     rows,
     slope,
     hid,
@@ -93,10 +91,10 @@
     dlog,
     dres,
     grad,
-    from_y,
-    from_x,
-    last_x,
-    last_y,
+    from_core,
+    from_pair,
+    last,
+    power,
     sums,
     spans,
     late,
@@ -105,12 +103,16 @@
     recv_sem,
 ):
     ci, me = lax.axis_index("chain"), lax.axis_index("dp")
-    gy, gx = grid_of(n)
-    my, mx = me // gx, lax.rem(me, gx)
+    pairs = n // 2
+    core, side = lax.rem(ci, 2), lax.rem(me, 2)
+    pair = me // 2
+    leads = core == side
+    moves = core != side
+    cross = (ci + 1 - 2 * core, me + 1 - 2 * side)
+    twin = (ci + 1 - 2 * core, me)
     block, width = own.shape[1], own.shape[2]
     depth = n * block
-    half = block // 2
-    step = min(32, half)
+    step = min(32, block)
     batch = rows.shape[0]
     tiles = width // TILE
     factor = (depth**-0.5, width**-0.5, depth**-0.5)
@@ -130,14 +132,8 @@
         )
         return copy
 
-    def dp_peer(y, x):
-        return (ci, y * gx + x)
-
-    def y_at(d):
-        return lax.rem(my + d, gy)
-
-    def x_at(d):
-        return lax.rem(mx + d, gx)
+    def pair_at(d):
+        return lax.rem(pair + d, pairs)
 
     barrier = pltpu.get_barrier_semaphore()
     for d in range(1, n):
@@ -148,6 +144,8 @@
         pl.semaphore_signal(
             barrier, inc=1, device_id=(lax.rem(ci + d, c), me), device_id_type=pl.DeviceIdType.MESH
         )
+
+    pl.semaphore_signal(barrier, inc=1, device_id=cross, device_id_type=pl.DeviceIdType.MESH)
 
     end = jnp.where(ci == 0, 0, 1)
     loads = [
@@ -178,9 +176,13 @@
         def body(r, _):
             off = pl.multiple_of(r * step, step)
             value = own[m, pl.ds(off, step), :]
-            wide[m, pl.ds(pl.multiple_of(me * block + off, step), step), :] = (
-                value * factor[m]
-            ).astype(BF16)
+            low = (value * factor[m]).astype(BF16)
+            stage[m, pl.ds(off, step), :] = low
+
+            @pl.when(leads)
+            def _():
+                wide[m, pl.ds(pl.multiple_of(me * block + off, step), step), :] = low
+
             near[m, pl.ds(off, step), :] = value.astype(BF16)
             return 0
 
@@ -191,15 +193,15 @@
         lowered(m)
     blanked(0)
     blanked(1)
-    pl.semaphore_wait(barrier, n - 1 + c - 1)
+    pl.semaphore_wait(barrier, n - 1 + c - 1 + 1)
 
     def column(t):
         return pl.ds(pl.multiple_of(t * TILE, TILE), TILE)
 
     everything = pl.ds(0, width)
 
-    def piece(ref, m, index, h, at=everything):
-        return ref.at[m, pl.ds(pl.multiple_of(index * block + h * half, half), half), at]
+    def piece(ref, m, index, at=everything):
+        return ref.at[m, pl.ds(pl.multiple_of(index * block, block), block), at]
 
     started = []
 
@@ -208,48 +210,83 @@
         started.append(copy)
         return copy
 
-    first, own_far, second = {}, {}, {}
+    hop, across, over = {}, {}, {}
+
+    def swap(src, dst):
+        copy = remote(src, dst, cross)
+
+        @pl.when(moves)
+        def _():
+            copy.start()
+
+        swapped.append(copy)
+        return copy
+
+    def arrive(copy):
+        @pl.when(moves)
+        def _():
+            copy.wait_recv()
+
+    swapped = []
 
     def send_own(key, m, at=everything):
-        a, b = piece(wide, m, me, 0, at), piece(wide, m, me, 1, at)
-        first[key] = (
-            [begin(remote(a, a, dp_peer(my, x_at(d)))) for d in range(1, gx)],
-            [begin(remote(b, b, dp_peer(y_at(d), mx))) for d in range(1, gy)],
-        )
-        own_far[key] = [begin(remote(a, a, dp_peer(y_at(d), mx))) for d in range(1, gy)] + [
-            begin(remote(b, b, dp_peer(my, x_at(d)))) for d in range(1, gx)
+        hop[key] = swap(stage.at[m, :, at], piece(wide, m, me, at))
+
+    def spread(key, m, at=everything):
+        arrive(hop[key])
+        held = piece(wide, m, 2 * pair + core, at)
+        across[key] = [
+            begin(remote(held, held, (ci, 2 * pair_at(d) + side))) for d in range(1, pairs)
         ]
+        over[key] = [begin(remote(held, held, twin))]
 
     def forward(key, m, at=everything):
-        second[key] = []
-        for d in range(1, gx):
-            first[key][0][d - 1].wait_recv()
-            a = piece(wide, m, my * gx + x_at(gx - d), 0, at)
-            for e in range(1, gy):
-                second[key].append(begin(remote(a, a, dp_peer(y_at(e), mx))))
-        for d in range(1, gy):
-            first[key][1][d - 1].wait_recv()
-            b = piece(wide, m, y_at(gy - d) * gx + mx, 1, at)
-            for e in range(1, gx):
-                second[key].append(begin(remote(b, b, dp_peer(my, x_at(e)))))
+        for d in range(1, pairs):
+            across[key][d - 1].wait_recv()
+            held = piece(wide, m, 2 * pair_at(pairs - d) + core, at)
+            over[key].append(begin(remote(held, held, twin)))
 
     def gathered(key):
-        for copy in own_far[key] + second[key]:
+        for copy in over[key]:
             copy.wait_recv()
 
-    def send_chunk(t):
-        if t < tiles:
-            send_own((2, t), 2, pl.ds(t * TILE, TILE))
-
-    def forward_chunk(t):
-        if t < tiles:
-            forward((2, t), 2, pl.ds(t * TILE, TILE))
+    def chunk(step_of, t):
+        step_of((2, t), 2, pl.ds(t * TILE, TILE))
 
     send_own(0, 0)
+
+    lab_rows = jnp.broadcast_to(labs[...], (8, batch))
+    lab_out[...] = lab_rows
+
+    @pl.when(leads)
+    def _():
+        lab_in[...] = lab_rows
+
+    row_of = jnp.broadcast_to(picks[...], (LANES, batch)).T
+    lane = lax.broadcasted_iota(jnp.int32, (batch, LANES), 1)
+    for k in range(pool_v.shape[0] // LANES):
+        hot[:, k * LANES : (k + 1) * LANES] = (row_of == lane + k * LANES).astype(F32).astype(BF16)
+    loads[3].wait()
+
+    @pl.loop(0, tiles)
+    def _(t):
+        at = column(t)
+        picked = dot_nn(hot[...], pool_v[:, at]).astype(BF16)
+        rows_out[:, at] = picked
+
+        @pl.when(leads)
+        def _():
+            rows[:, at] = picked
+
+    lab_swap = swap(lab_out, lab_in)
+    row_swap = swap(rows_out, rows)
     send_own(1, 1)
     loads[2].wait()
     turned(own.at[2], 0)
     lowered(2)
+    spread(0, 0)
+    for t in range(tiles):
+        chunk(send_own, t)
     ups = [remote(near.at[m], before.at[m], (lax.rem(ci + 1, c), me)) for m in range(3)]
     downs = [remote(near.at[m], after.at[m], (lax.rem(ci + c - 1, c), me)) for m in range(3)]
     has_next, has_prev = ci < c - 1, ci > 0
@@ -264,22 +301,17 @@
         for copy in downs:
             copy.start()
 
-    row_of = jnp.broadcast_to(picks[...], (LANES, batch)).T
-    lab_t[...] = jnp.broadcast_to(labs[...], (LANES, batch)).T
-    lane = lax.broadcasted_iota(jnp.int32, (batch, LANES), 1)
-    for k in range(pool_v.shape[0] // LANES):
-        hot[:, k * LANES : (k + 1) * LANES] = (row_of == lane + k * LANES).astype(F32).astype(BF16)
-    loads[3].wait()
+    forward(0, 0)
+    arrive(lab_swap)
+    lab_t[...] = jnp.broadcast_to(lab_in[...][0:1, :], (LANES, batch)).T
+    arrive(row_swap)
 
     @pl.loop(0, tiles)
     def _(t):
         at = column(t)
-        picked = dot_nn(hot[...], pool_v[:, at]).astype(BF16)
-        rows[:, at] = picked
-        rows_t[at, :] = picked.T
-
-    forward(0, 0)
-    send_chunk(0)
+        rows_t[at, :] = rows[:, at].T
+
+    spread(1, 1)
 
     for load in loads[4:]:
         load.wait()
@@ -324,8 +356,7 @@
         begin(remote(sums.at[me], sums.at[me], (ci, lax.rem(me + d, n)))) for d in range(1, n)
     ]
 
-    forward(1, 1)
-    send_chunk(1)
+    chunk(spread, 0)
     gathered(0)
 
     @pl.loop(0, tiles)
@@ -338,8 +369,9 @@
         hid_t[at, :] = value.T
         slope[:, at] = sig * (1.0 + pre * (1.0 - sig))
 
-    forward_chunk(0)
-    send_chunk(2)
+    forward(1, 1)
+    for t in range(1, tiles):
+        chunk(spread, t)
 
     for copy in sums_out:
         copy.wait_recv()
@@ -350,13 +382,13 @@
             total = total + ref[j, k]
         return whole(total)
 
-    sq_ahead, sq_behind, cross = (over_dp(sums, k) for k in range(3))
+    sq_ahead, sq_behind, mixed = (over_dp(sums, k) for k in range(3))
     len_ahead = jnp.sqrt(sq_ahead + EPS)
     len_behind = jnp.sqrt(sq_behind + EPS)
     raw_sq = (
         sq_ahead / (len_ahead * len_ahead)
         + sq_behind / (len_behind * len_behind)
-        + 2.0 * cross / (len_ahead * len_behind)
+        + 2.0 * mixed / (len_ahead * len_behind)
     )
     raw_len = jnp.sqrt(raw_sq + EPS)
     spans[ci, 0] = jnp.broadcast_to(len_behind, (8, LANES))
@@ -374,8 +406,7 @@
         resid[:, at] = value
         resid_t[at, :] = value.T
 
-    forward_chunk(1)
-    send_chunk(3)
+    chunk(forward, 0)
 
     def classify(t, energy):
         at = column(t)
@@ -395,68 +426,60 @@
             at = column(t)
             grad[m, at, :] = dot_nn(left_t[at, :], right[...]).astype(BF16)
 
-    to_rows, to_cols, back_x, back_y = {}, {}, {}, {}
+    to_core, to_pair, to_home = {}, {}, {}
 
     def scatter(m, at=everything):
-        to_rows.setdefault(m, [])
-        to_cols.setdefault(m, [])
-        for d in range(1, gy):
-            for x in range(gx):
-                to_rows[m].append(
-                    begin(
-                        remote(
-                            piece(grad, m, y_at(d) * gx + x, 0, at),
-                            from_y.at[m, d - 1, x, :, at],
-                            dp_peer(y_at(d), mx),
-                        )
+        to_core.setdefault(m, [])
+        for q in range(pairs):
+            to_core[m].append(
+                begin(
+                    remote(
+                        piece(grad, m, 2 * q + 1 - core, at), from_core.at[m, q, :, at], twin
                     )
                 )
-        for d in range(1, gx):
-            for y in range(gy):
-                to_cols[m].append(
-                    begin(
-                        remote(
-                            piece(grad, m, y * gx + x_at(d), 1, at),
-                            from_x.at[m, d - 1, y, :, at],
-                            dp_peer(my, x_at(d)),
-                        )
-                    )
-                )
-
-    def combine(m, index, h, arrived, count, slot):
-        def body(r, _):
+            )
+
+    def combine(m, into, index, parts):
+        @pl.loop(0, block // step)
+        def _(r):
             off = pl.multiple_of(r * step, step)
-            at = pl.ds(pl.multiple_of(index * block + h * half + off, step), step)
+            at = pl.ds(pl.multiple_of(index * block + off, step), step)
             total = grad[m, at, :].astype(F32)
-            for d in range(count):
-                total = total + arrived[m, d, slot, pl.ds(off, step), :].astype(F32)
-            grad[m, at, :] = total.astype(BF16)
-            return 0
-
-        lax.fori_loop(0, half // step, body, 0)
+            for part in parts:
+                total = total + part[pl.ds(off, step), :].astype(F32)
+            into[pl.ds(off, step), :] = total.astype(BF16)
 
     def scatter_on(m):
-        for copy in to_rows[m]:
+        for copy in to_core[m]:
             copy.wait_recv()
-        back_x[m] = []
-        for d in range(1, gx):
-            index = my * gx + x_at(d)
-            combine(m, index, 0, from_y, gy - 1, x_at(d))
-            back_x[m].append(
-                begin(remote(piece(grad, m, index, 0), last_x.at[m, d - 1], dp_peer(my, x_at(d))))
-            )
-        for copy in to_cols[m]:
+        to_pair[m] = []
+        for d in range(1, pairs):
+            q = pair_at(d)
+            held = piece(grad, m, 2 * q + core)
+            combine(m, held, 2 * q + core, [from_core.at[m, q]])
+            to_pair[m].append(begin(remote(held, from_pair.at[m, d - 1], (ci, 2 * q + side))))
+
+    def scatter_home(m):
+        for copy in to_pair[m]:
             copy.wait_recv()
-        back_y[m] = []
-        for d in range(1, gy):
-            index = y_at(d) * gx + mx
-            combine(m, index, 1, from_x, gx - 1, y_at(d))
-            back_y[m].append(
-                begin(remote(piece(grad, m, index, 1), last_y.at[m, d - 1], dp_peer(y_at(d), mx)))
-            )
+        parts = [from_core.at[m, pair]] + [from_pair.at[m, d] for d in range(pairs - 1)]
+        held = piece(grad, m, 2 * pair + core)
+        combine(m, held, 2 * pair + core, parts)
+
+        @pl.when(leads)
+        def _():
+            @pl.loop(0, block // step)
+            def _(r):
+                off = pl.multiple_of(r * step, step)
+                at = pl.ds(pl.multiple_of(me * block + off, step), step)
+                last[m, pl.ds(off, step), :] = grad[m, at, :]
+
+        to_home[m] = swap(held, last.at[m])
 
     energy = zero
     for t in range(tiles):
+        if t + 1 < tiles:
+            chunk(forward, t + 1)
         gathered((2, t))
         energy = classify(t, energy)
         at = pl.ds(t * TILE, TILE)
@@ -466,8 +489,6 @@
             of = column(r)
             grad[2, of, at] = dot_nn(resid_t[of, :], dlog[:, at]).astype(BF16)
 
-        forward_chunk(t + 2)
-        send_chunk(t + 4)
         scatter(2, at)
 
     @pl.loop(0, depth // TILE)
@@ -477,6 +498,7 @@
 
     products(1, hid_t, dres)
     scatter(1)
+    scatter_on(2)
 
     @pl.loop(0, depth // TILE)
     def _(t):
@@ -485,6 +507,9 @@
 
     products(0, rows_t, dlog)
     scatter(0)
+    scatter_on(1)
+    power[0] = energy * (0.5 * norm)
+    power_swap = swap(power.at[0], power.at[1])
 
     for copy in spans_out:
         copy.wait_recv()
@@ -509,40 +534,28 @@
         band = band + length
     band = band + spans[c - 1, 1, 0:1, 0:1]
 
+    scatter_on(0)
     for m in (2, 1, 0):
-        scatter_on(m)
+        scatter_home(m)
+    arrive(power_swap)
 
     def finish(m, carry):
-        for copy in back_x[m] + back_y[m]:
-            copy.wait_recv()
-        for h, arrived, count, slot, last, lasts in (
-            (0, from_y, gy - 1, mx, last_x, gx - 1),
-            (1, from_x, gx - 1, my, last_y, gy - 1),
-        ):
-
-            def body(r, carry):
-                off = pl.multiple_of(r * step, step)
-                total = grad[
-                    m, pl.ds(pl.multiple_of(me * block + h * half + off, step), step), :
-                ].astype(F32)
-                for d in range(count):
-                    total = total + arrived[m, d, slot, pl.ds(off, step), :].astype(F32)
-                for d in range(lasts):
-                    total = total + last[m, d, pl.ds(off, step), :].astype(F32)
-                total = total * factor[m]
-                at = pl.ds(h * half + off, step)
-                edge[m, at, :] = total
-                return carry[0] + fold(total * tau[m, at, :]), carry[1] + fold(total * total)
-
-            carry = lax.fori_loop(0, half // step, body, carry)
-        return carry
+        arrive(to_home[m])
+
+        def body(r, carry):
+            at = pl.ds(pl.multiple_of(r * step, step), step)
+            total = last[m, at, :].astype(F32) * factor[m]
+            edge[m, at, :] = total
+            return carry[0] + fold(total * tau[m, at, :]), carry[1] + fold(total * total)
+
+        return lax.fori_loop(0, block // step, body, carry)
 
     carry = (zero, zero)
     for m in (2, 1, 0):
         carry = finish(m, carry)
     late[me, 0] = carry[0]
     late[me, 1] = carry[1]
-    late[me, 2] = energy * (0.5 * norm)
+    late[me, 2] = jnp.where(leads, power[0], power[1])
     late_out = [
         begin(remote(late.at[me], late.at[me], (ci, lax.rem(me + d, n)))) for d in range(1, n)
     ]
@@ -591,6 +604,11 @@
     @pl.when(has_prev)
     def _():
         for copy in downs:
+            copy.wait_send()
+
+    @pl.when(moves)
+    def _():
+        for copy in swapped:
             copy.wait_send()
 
     for copy in started:
@@ -616,9 +634,8 @@
     block, width = images_in.shape[1], images_in.shape[2]
     classes = images_out.shape[2]
     depth = n * block
-    half = block // 2
     batch = batch_rows.shape[1]
-    gy, gx = grid_of(n)
+    pairs = n // 2
     copies = copies_of(n, c, width // TILE)
     vmem = pl.BlockSpec(memory_space=pltpu.VMEM)
     anywhere = pl.BlockSpec(memory_space=pl.ANY)
@@ -645,9 +662,13 @@
             pltpu.VMEM((3, block, width), BF16),
             pltpu.VMEM((3, block, width), BF16),
             pltpu.VMEM((3, block, width), BF16),
+            pltpu.VMEM((3, block, width), BF16),
             pltpu.VMEM(data_pool.shape, BF16),
             pltpu.VMEM((batch, data_pool.shape[0]), BF16),
             pltpu.VMEM((batch, LANES), jnp.int32),
+            pltpu.VMEM((8, batch), jnp.int32),
+            pltpu.VMEM((8, batch), jnp.int32),
+            pltpu.VMEM((batch, depth), BF16),
             pltpu.VMEM((batch, depth), BF16),
             pltpu.VMEM((batch, width), F32),
             pltpu.VMEM((batch, width), BF16),
@@ -658,10 +679,10 @@
             pltpu.VMEM((batch, width), BF16),
             pltpu.VMEM((batch, depth), BF16),
             pltpu.VMEM((3, depth, width), BF16),
-            pltpu.VMEM((3, max(gy - 1, 1), gx, half, width), BF16),
-            pltpu.VMEM((3, max(gx - 1, 1), gy, half, width), BF16),
-            pltpu.VMEM((3, max(gx - 1, 1), half, width), BF16),
-            pltpu.VMEM((3, max(gy - 1, 1), half, width), BF16),
+            pltpu.VMEM((3, pairs, block, width), BF16),
+            pltpu.VMEM((3, max(pairs - 1, 1), block, width), BF16),
+            pltpu.VMEM((3, block, width), BF16),
+            pltpu.VMEM((2, 8, LANES), F32),
             pltpu.VMEM((n, 3, 8, LANES), F32),
             pltpu.VMEM((c, 2, 8, LANES), F32),
             pltpu.VMEM((n, 3, 8, LANES), F32),

time: 131 us -> 131 us (level)
  no operation moved by 1% of the time
where the time goes in v3:
time: 131 us; the launch traced here: 130 us
  Pallas kernels  119 us (91%)
  between operations  6.5 us (5%)
  local copies, waits for them, and re-layouts  4.39 us (3%)
    pallas_call x1, Pallas kernels, on_device(): pl.pallas_call(functools.partial(kernel, n, c, classes), out_shape=(jax.S...  119 us
    unnamed x7, local copies, waits for them, and re-layouts  4.39 us

profile of v3, /device:TPU:0, one launch (start us, length us, event | category | flops | bytes accessed | tf_op | source)
XLA Modules:
  0.0 129.8 jit_solution(10048887087162746959)
XLA Ops:
  1.3 118.9 %shard_map.145 = (f32[1,256,1024]{2,1,0:T(8,128)}, f32[1,256,1024]{2,1,0:T(8,128)}, f32[1,1000,256]{2,1,0:T(8,128)}, f32[1]{0:T(128)}, f32[1]{0:T(128)}, /*index=5*/f32[1]{0:T(128)}) custom-call(f32[1,256,1024]{2,1,0:T(8,128)} %p_in.1, f32[1,256,1024]{2,1,0:T(8,128)} %p_mid.1, f32[1,1000,256]{2,1,0:T(8,128)} %bitcast.4, f32[2,256,1024]{2,1,0:T(8,128)} %e_in.1, ...), custom_call_target="tpu_custom_call" | custom-call | tf_op jit(solution)/shard_map/pallas_call | solution.py:644
  120.1 0.0 copy-start
  120.2 0.0 copy-start.1
  120.2 2.5 %copy.23 = f32[1,256,1024]{2,1,0:T(8,128)} copy(f32[1,256,1024]{2,1,0:T(8,128)} %get-tuple-element.24) | data formatting | bytes 2097152
  122.6 0.0 copy-done
  122.6 1.0 copy.24
  123.6 0.0 copy-done.1
  123.6 1.0 copy.25
Async XLA Ops:
  120.1 2.5 %copy-start = (f32[1,256,1024]{2,1,0:T(8,128)S(1)}, f32[1,256,1024]{2,1,0:T(8,128)}, u32[]{:S(2)}) copy-start(f32[1,256,1024]{2,1,0:T(8,128)} %get-tuple-element.25) | copy-start | bytes 3145732
  120.2 3.4 %copy-start.1 = (f32[1,1000,256]{2,1,0:T(8,128)S(1)}, f32[1,1000,256]{2,1,0:T(8,128)}, u32[]{:S(2)}) copy-start(f32[1,1000,256]{2,1,0:T(8,128)} %get-tuple-element.14) | copy-start | bytes 3072004

commit v4 on v3

--- a/solution.py
+++ b/solution.py
@@ -19,7 +19,7 @@
     pairs = count // 2
     gather = 1 + (pairs - 1) + pairs
     scatter = pairs
-    return (2 + chunks) * (gather + scatter) + 3 * pairs + 2 * (count - 1) + (chain - 1) + 9
+    return (2 + chunks) * (gather + scatter + pairs) + 3 + 2 * (count - 1) + (chain - 1) + 9
 
 
 def dot_nn(left, right):
@@ -302,17 +302,6 @@
             copy.start()
 
     forward(0, 0)
-    arrive(lab_swap)
-    lab_t[...] = jnp.broadcast_to(lab_in[...][0:1, :], (LANES, batch)).T
-    arrive(row_swap)
-
-    @pl.loop(0, tiles)
-    def _(t):
-        at = column(t)
-        rows_t[at, :] = rows[:, at].T
-
-    spread(1, 1)
-
     for load in loads[4:]:
         load.wait()
     turned(edge.at[2], 1)
@@ -356,7 +345,15 @@
         begin(remote(sums.at[me], sums.at[me], (ci, lax.rem(me + d, n)))) for d in range(1, n)
     ]
 
-    chunk(spread, 0)
+    arrive(lab_swap)
+    lab_t[...] = jnp.broadcast_to(lab_in[...][0:1, :], (LANES, batch)).T
+    arrive(row_swap)
+
+    @pl.loop(0, tiles)
+    def _(t):
+        at = column(t)
+        rows_t[at, :] = rows[:, at].T
+
     gathered(0)
 
     @pl.loop(0, tiles)
@@ -369,6 +366,8 @@
         hid_t[at, :] = value.T
         slope[:, at] = sig * (1.0 + pre * (1.0 - sig))
 
+    spread(1, 1)
+    chunk(spread, 0)
     forward(1, 1)
     for t in range(1, tiles):
         chunk(spread, t)
@@ -428,36 +427,33 @@
 
     to_core, to_pair, to_home = {}, {}, {}
 
-    def scatter(m, at=everything):
-        to_core.setdefault(m, [])
-        for q in range(pairs):
-            to_core[m].append(
-                begin(
-                    remote(
-                        piece(grad, m, 2 * q + 1 - core, at), from_core.at[m, q, :, at], twin
-                    )
-                )
-            )
-
-    def combine(m, into, index, parts):
+    def scatter(key, m, at=everything):
+        to_core[key] = [
+            begin(remote(piece(grad, m, 2 * q + 1 - core, at), from_core.at[m, q, :, at], twin))
+            for q in range(pairs)
+        ]
+
+    def combine(m, into, index, parts, cols=everything):
         @pl.loop(0, block // step)
         def _(r):
             off = pl.multiple_of(r * step, step)
             at = pl.ds(pl.multiple_of(index * block + off, step), step)
-            total = grad[m, at, :].astype(F32)
+            total = grad[m, at, cols].astype(F32)
             for part in parts:
                 total = total + part[pl.ds(off, step), :].astype(F32)
             into[pl.ds(off, step), :] = total.astype(BF16)
 
-    def scatter_on(m):
-        for copy in to_core[m]:
+    def scatter_on(key, m, at=everything):
+        for copy in to_core[key]:
             copy.wait_recv()
-        to_pair[m] = []
+        to_pair.setdefault(m, [])
         for d in range(1, pairs):
             q = pair_at(d)
-            held = piece(grad, m, 2 * q + core)
-            combine(m, held, 2 * q + core, [from_core.at[m, q]])
-            to_pair[m].append(begin(remote(held, from_pair.at[m, d - 1], (ci, 2 * q + side))))
+            held = piece(grad, m, 2 * q + core, at)
+            combine(m, held, 2 * q + core, [from_core.at[m, q, :, at]], at)
+            to_pair[m].append(
+                begin(remote(held, from_pair.at[m, d - 1, :, at], (ci, 2 * q + side)))
+            )
 
     def scatter_home(m):
         for copy in to_pair[m]:
@@ -489,27 +485,33 @@
             of = column(r)
             grad[2, of, at] = dot_nn(resid_t[of, :], dlog[:, at]).astype(BF16)
 
-        scatter(2, at)
+        scatter((2, t), 2, at)
+        if t > 0:
+            chunk(scatter_on, t - 1)
 
     @pl.loop(0, depth // TILE)
     def _(t):
         at = column(t)
         dres[:, at] = dot_nt(dlog[...], wide[2, at, :]).astype(BF16)
 
+    chunk(scatter_on, tiles - 1)
+
     products(1, hid_t, dres)
-    scatter(1)
-    scatter_on(2)
+    scatter(1, 1)
 
     @pl.loop(0, depth // TILE)
     def _(t):
         at = column(t)
         dlog[:, at] = (dot_nt(dres[...], wide[1, at, :]) * slope[:, at]).astype(BF16)
 
+    scatter_on(1, 1)
     products(0, rows_t, dlog)
-    scatter(0)
-    scatter_on(1)
+    scatter(0, 0)
     power[0] = energy * (0.5 * norm)
     power_swap = swap(power.at[0], power.at[1])
+
+    scatter_on(0, 0)
+    scatter_home(2)
 
     for copy in spans_out:
         copy.wait_recv()
@@ -534,8 +536,7 @@
         band = band + length
     band = band + spans[c - 1, 1, 0:1, 0:1]
 
-    scatter_on(0)
-    for m in (2, 1, 0):
+    for m in (1, 0):
         scatter_home(m)
     arrive(power_swap)
 

time: 131 us -> 127 us (0.969)
  Pallas kernels: 119 us -> 114 us
    pallas_call x1, Pallas kernels: 119 us -> 114 us  [on_device(): pl.pallas_call(functools.partial(kernel, n, c, classes), out_shape=(jax.S...]
where the time goes in v4:
time: 127 us; the launch traced here: 125 us
  Pallas kernels  114 us (90%)
  between operations  6.5 us (5%)
  local copies, waits for them, and re-layouts  4.39 us (3%)
    pallas_call x1, Pallas kernels, on_device(): pl.pallas_call(functools.partial(kernel, n, c, classes), out_shape=(jax.S...  114 us
    unnamed x7, local copies, waits for them, and re-layouts  4.39 us

profile of v4, /device:TPU:0, one launch (start us, length us, event | category | flops | bytes accessed | tf_op | source)
XLA Modules:
  0.0 125.3 jit_solution(4062360949744338251)
XLA Ops:
  1.3 114.4 %shard_map.145 = (f32[1,256,1024]{2,1,0:T(8,128)}, f32[1,256,1024]{2,1,0:T(8,128)}, f32[1,1000,256]{2,1,0:T(8,128)}, f32[1]{0:T(128)}, f32[1]{0:T(128)}, /*index=5*/f32[1]{0:T(128)}) custom-call(f32[1,256,1024]{2,1,0:T(8,128)} %p_in.1, f32[1,256,1024]{2,1,0:T(8,128)} %p_mid.1, f32[1,1000,256]{2,1,0:T(8,128)} %bitcast.4, f32[2,256,1024]{2,1,0:T(8,128)} %e_in.1, ...), custom_call_target="tpu_custom_call" | custom-call | tf_op jit(solution)/shard_map/pallas_call | solution.py:645
  115.7 0.0 copy-start
  115.7 0.0 copy-start.1
  115.7 2.5 %copy.23 = f32[1,256,1024]{2,1,0:T(8,128)} copy(f32[1,256,1024]{2,1,0:T(8,128)} %get-tuple-element.24) | data formatting | bytes 2097152
  118.2 0.0 copy-done
  118.2 1.0 copy.24
  119.1 0.0 copy-done.1
  119.1 1.0 copy.25
Async XLA Ops:
  115.7 2.5 %copy-start = (f32[1,256,1024]{2,1,0:T(8,128)S(1)}, f32[1,256,1024]{2,1,0:T(8,128)}, u32[]{:S(2)}) copy-start(f32[1,256,1024]{2,1,0:T(8,128)} %get-tuple-element.25) | copy-start | bytes 3145732
  115.7 3.4 %copy-start.1 = (f32[1,1000,256]{2,1,0:T(8,128)S(1)}, f32[1,1000,256]{2,1,0:T(8,128)}, u32[]{:S(2)}) copy-start(f32[1,1000,256]{2,1,0:T(8,128)} %get-tuple-element.14) | copy-start | bytes 3072004
